TPU v7x, 256 devices: a whole 4x4x8 slice. The times are simulated.
256 devices in a mesh: rep: 32 (over y_hi, z, core), tp: 8 (over y_lo, x).
Axes of the slice: x: 4, y: 4 (y_hi: 2, y_lo: 2; y = y_hi * 2 + y_lo), z: 8, core: 2. Of those that a mesh axis runs over, the one named last changes fastest.
Arguments:
- queries: bfloat16 [8192, 8192], P('rep', 'tp'), may hold values from -8 to 8
- cand_keys: bfloat16 [8192, 1024], P('rep', 'tp'), may hold values from -6 to 6
- cand_values: bfloat16 [8192, 1024], P('rep', 'tp'), may hold values from -6 to 6
- prefix_kv: bfloat16 [32, 2, 4096, 1024], P('rep', None, None, 'tp'), may hold values from -8 to 8
- owner: int32 [1], replicated, may hold values from 0 to 31
- lengths: int32 [32, 2], P('rep'), may hold values from 1 to 128, as said below
- out_weight: bfloat16 [8192, 4096], P('tp'), may hold values from -2.390625 to 2.390625
Outputs:
- attn_out: bfloat16 [8192, 4096], P(('rep', 'tp'))
Inputs may be any that keep to these rules, and one draw needn't show every extreme that they name: Only the slice of prefix_kv at index owner[0] is read. Candidate c of group g has its real tokens in its first lengths[g, c] slots; the rest are padding.
All inputs are finite; a program needn't handle non-finite values.
Results may differ from a plain program's by a relative error of at most 0.017.
Values may be sent and summed in bfloat16 or wider, within the bound.
No kernel may reach another device: no remote copies, remote signals or barrier semaphores. Data moves between devices by JAX's collectives and lax.ppermute only.
A program may use at most 64 MiB of HBM per device.

v0:
```python
import functools
import math

import jax
import jax.numpy as jnp
from jax import lax
from jax.experimental import pallas as pl
from jax.experimental.pallas import tpu as pltpu
from jax.sharding import PartitionSpec as P

HEADS = 8
HD = 128
CLEN = 128
PIECE = 256
NEG = -1e30
SCALE = math.log2(math.e) / math.sqrt(HD)


REP = [(y, z, c) for y in range(2) for z in range(8) for c in range(2)]
TP = [(y, x) for y in range(2) for x in range(4)]


def rep_id(y, z, c):
    return y * 16 + (z % 8) * 2 + c


def tp_id(y, x):
    return y * 4 + x % 4


CORE_SWAP = [(rep_id(*r), rep_id(r[0], r[1], 1 - r[2])) for r in REP]
YHI_SWAP = [(rep_id(*r), rep_id(1 - r[0], r[1], r[2])) for r in REP]
YLO_SWAP = [(tp_id(y, x), tp_id(1 - y, x)) for y, x in TP]


def z_shift(d):
    return [(rep_id(y, z, c), rep_id(y, z + d, c)) for y, z, c in REP]


def x_shift(d):
    return [(tp_id(y, x), tp_id(y, x + d)) for y, x in TP]


def lanes(s):
    return [s[:, i * 128 : (i + 1) * 128] for i in range(s.shape[1] // 128)]


def absorb(q, keys, values, masks, m_old, acc_old):
    cols = []
    for k, mask in zip(keys, masks):
        s = lanes(lax.dot_general(q, k, (((1,), (1,)), ((), ())), preferred_element_type=jnp.float32))
        if mask is not None:
            s = [jnp.where(ok, t, NEG) for ok, t in zip(mask, s)]
        cols += s
    top = jnp.max(functools.reduce(jnp.maximum, cols), axis=1, keepdims=True)
    m_new = jnp.broadcast_to(top, (q.shape[0], 128)) if m_old is None else jnp.maximum(m_old, top)
    shift = m_new * SCALE
    p = jnp.concatenate([jnp.exp2(t * SCALE - shift).astype(jnp.bfloat16) for t in cols], axis=1)
    v = jnp.concatenate(values, axis=0)
    v = jnp.concatenate([v, jnp.ones(v.shape, jnp.bfloat16)], axis=1)
    pv = jnp.dot(p, v, preferred_element_type=jnp.float32)
    if m_old is None:
        return m_new, pv
    decay = jnp.exp2(m_old * SCALE - shift)
    return m_new, acc_old * jnp.concatenate([decay, decay], axis=1) + pv


def pieces(refs):
    keys = [r[j, 0] for r in refs for j in range(r.shape[0])]
    values = [r[j, 1] for r in refs for j in range(r.shape[0])]
    return keys, values


UNROLL = 8


def each_head(f):
    def step(i, carry):
        for j in range(UNROLL):
            f(i * UNROLL + j)
        return carry

    lax.fori_loop(0, HEADS // UNROLL, step, 0)


def head_cols(h):
    return pl.ds(pl.multiple_of(h * HD, HD), HD)


def first_kernel(lens, q_ref, ck, cv, a0, m_out, acc_out):
    rows = q_ref.shape[0]

    def head(h):
        keys, values = pieces([a0])
        slot = lax.broadcasted_iota(jnp.int32, (rows, 128), 0) // CLEN
        lane = lax.broadcasted_iota(jnp.int32, (rows, 128), 1)
        mask = [(slot == t) & (lane < lens[t]) for t in range(2)]
        q = q_ref[:, head_cols(h)]
        m_out[h], acc_out[h] = absorb(
            q, [ck[...]] + keys, [cv[...]] + values, [mask] + [None] * len(keys), None, None
        )

    each_head(head)


def mid_kernel(n, q_ref, *refs):
    m_in, acc_in, m_out, acc_out = refs[n:]

    def head(h):
        keys, values = pieces(refs[:n])
        q = q_ref[:, head_cols(h)]
        m_out[h], acc_out[h] = absorb(q, keys, values, [None] * len(keys), m_in[h], acc_in[h])

    each_head(head)


W_BLOCK = 512


def last_kernel(n, spot, q_ref, *refs):
    m_in, acc_in, w, own_a, x1, x2, x3, own_b, yb, ctx = refs[n:]

    def head(h):
        keys, values = pieces(refs[:n])
        q = q_ref[:, head_cols(h)]
        _, acc = absorb(q, keys, values, [None] * len(keys), m_in[h], acc_in[h])
        ctx[:, head_cols(h)] = (acc[:, :HD] / acc[:, HD:]).astype(jnp.bfloat16)

    each_head(head)

    tile = own_a.shape[1]
    half = own_a.shape[2]
    tp_of = [((spot[0] + dy) % 2) * 4 + (spot[1] + dx) % 4 for dy in range(2) for dx in range(4)]
    rel = jnp.concatenate([ctx[pl.ds(pl.multiple_of(t * tile, tile), tile)] for t in tp_of], axis=0)

    def product(c):
        return jnp.dot(rel, w[:, pl.ds(c, W_BLOCK)], preferred_element_type=jnp.float32).astype(jnp.bfloat16)

    for c in range(0, half, W_BLOCK):
        y = product(half + c)
        for dy, ref in enumerate((own_b, yb)):
            for dx in range(4):
                ref[dx, :, pl.ds(c, W_BLOCK)] = y[(dy * 4 + dx) * tile : (dy * 4 + dx + 1) * tile]
        y = product(c)
        for dx, ref in enumerate((own_a, x1, x2, x3)):
            for dy in range(2):
                ref[dy, :, pl.ds(c, W_BLOCK)] = y[(dy * 4 + dx) * tile : (dy * 4 + dx + 1) * tile]


VM = pl.BlockSpec(memory_space=pltpu.VMEM)
SM = pl.BlockSpec(memory_space=pltpu.SMEM)


def cost(rows, keys, extra=0):
    return pl.CostEstimate(
        flops=4 * rows * HEADS * keys * HD + extra, transcendentals=rows * HEADS * keys, bytes_accessed=0
    )


def state_shapes(rows):
    return (
        jax.ShapeDtypeStruct((HEADS, rows, HD), jnp.float32),
        jax.ShapeDtypeStruct((HEADS, rows, 2 * HD), jnp.float32),
    )


def key_count(kvs):
    return sum(a.shape[0] for a in kvs) * PIECE


def first_call(lens, q, ck, cv, a0):
    rows = q.shape[0]
    return pl.pallas_call(
        first_kernel,
        out_shape=state_shapes(rows),
        in_specs=[SM] + [VM] * 4,
        out_specs=(VM, VM),
        cost_estimate=cost(rows, 2 * PIECE),
        compiler_params=pltpu.CompilerParams(vmem_limit_bytes=12 << 20),
        name="attn_first",
    )(lens, q, ck, cv, a0)


def mid_call(q, kvs, state):
    n = len(kvs)
    rows = q.shape[0]
    return pl.pallas_call(
        functools.partial(mid_kernel, n),
        out_shape=state_shapes(rows),
        in_specs=[VM] * (n + 3),
        out_specs=(VM, VM),
        input_output_aliases={n + 1: 0, n + 2: 1},
        cost_estimate=cost(rows, key_count(kvs)),
        compiler_params=pltpu.CompilerParams(vmem_limit_bytes=12 << 20),
        name="attn_mid",
    )(q, *kvs, *state)


def last_call(spot, q, kvs, state, w):
    n = len(kvs)
    rows = q.shape[0]
    part = lambda k: jax.ShapeDtypeStruct((k, rows // 8, w.shape[1] // 2), jnp.bfloat16)
    outs = (part(2), part(2), part(2), part(2), part(4), part(4))
    return pl.pallas_call(
        functools.partial(last_kernel, n),
        out_shape=outs,
        in_specs=[SM] + [VM] * (n + 4),
        out_specs=(VM,) * len(outs),
        scratch_shapes=[pltpu.VMEM((rows, w.shape[0]), jnp.bfloat16)],
        cost_estimate=cost(rows, key_count(kvs), 2 * rows * w.shape[0] * w.shape[1]),
        compiler_params=pltpu.CompilerParams(vmem_limit_bytes=12 << 20),
        name="attn_last",
    )(spot, q, *kvs, *state, w)


def f32(a):
    return a.astype(jnp.float32)


def reduce_rows(own_a, x1, x2, x3, own_b, yb):
    over_tp = functools.partial(lax.ppermute, axis_name="tp")
    ry = over_tp(yb, perm=YLO_SWAP)
    r2 = over_tp(x2, perm=x_shift(2))
    r1 = over_tp(x1, perm=x_shift(1))
    r3 = over_tp(x3, perm=x_shift(-1))
    s = f32(own_a) + f32(r1) + f32(r3) + f32(r2)
    u = f32(own_b) + f32(ry)
    ub = u.astype(jnp.bfloat16)
    t2 = over_tp(ub[2], perm=x_shift(2))
    t1 = over_tp(ub[1], perm=x_shift(1))
    t3 = over_tp(ub[3], perm=x_shift(-1))
    ty = over_tp(s[1].astype(jnp.bfloat16), perm=YLO_SWAP)
    left = s[0] + f32(ty)
    right = u[0] + f32(t1) + f32(t3) + f32(t2)
    return jnp.concatenate([left, right], axis=1).astype(jnp.bfloat16)


def body(queries, cand_keys, cand_values, prefix_kv, owner, lengths, out_weight):
    rep = lax.axis_index("rep")
    my_yh, my_z, my_c = rep // 16, (rep // 2) % 8, rep % 2
    tp = lax.axis_index("tp")
    spot = jnp.stack([tp // 4, tp % 4]).astype(jnp.int32)
    root = owner[0]
    root_yh, root_z, root_c = root // 16, (root // 2) % 8, root % 2
    over_rep = functools.partial(lax.ppermute, axis_name="rep")

    prefix = prefix_kv[0]
    partner = over_rep(prefix, perm=CORE_SWAP)
    mine = my_c == root_c
    up = 1 - 2 * my_c
    pick = lambda start, size: jnp.where(
        mine,
        lax.dynamic_slice_in_dim(prefix, start, size, 1),
        lax.dynamic_slice_in_dim(partner, start, size, 1),
    )
    whole = lambda d: pick(((my_z + up * d) % 8) * 2 * PIECE, 2 * PIECE)
    opposite = pick(((my_z + 4) % 8) * 2 * PIECE + my_c * PIECE, PIECE)
    steps = (my_z - root_z) % 8
    steps = jnp.where(my_c == 0, steps, (8 - steps) % 8)

    def branch(b):
        def send(steps, own, *parts):
            got = {}
            for d in (3, 4, 2, 1):
                pairs = [
                    (rep_id(y, z, c), rep_id(y, z + (1 - 2 * c) * d, c))
                    for y in range(2)
                    for z in (b, b + 4)
                    for c in range(2)
                ]
                got[d] = over_rep(parts[d - 1], perm=pairs)
            got[4] = jnp.concatenate([got[4], got[4]], axis=1)
            return lax.select_n(jnp.minimum(steps, 4), own, got[1], got[2], got[3], got[4])

        return send

    slot = lax.switch(
        root_z % 4, [branch(b) for b in range(4)], steps, whole(0), whole(1), whole(2), whole(3), opposite
    )
    half_of = lambda a, c: lax.dynamic_slice_in_dim(a, c * PIECE, PIECE, 1)
    from_partner = over_rep(half_of(slot, 1 - my_c), perm=CORE_SWAP)
    piece = jnp.where(steps <= 4, half_of(slot, my_c), from_partner)
    across = over_rep(piece, perm=YHI_SWAP)
    a0 = jnp.where(my_yh == root_yh, piece, across)[None]
    a0, spot = lax.optimization_barrier((a0, spot))

    above = over_rep(a0, perm=z_shift(-1))
    below = over_rep(a0, perm=z_shift(1))
    facing = over_rep(a0, perm=z_shift(4))
    state = first_call(lengths[0], queries, cand_keys, cand_values, a0)
    above, below, facing, state = lax.optimization_barrier((above, below, facing, state))

    far_above = over_rep(jnp.concatenate([above, facing]), perm=z_shift(-1))
    far_below = over_rep(jnp.concatenate([below, facing]), perm=z_shift(1))
    near_other = over_rep(jnp.concatenate([a0, above, below, facing]), perm=CORE_SWAP)
    state = mid_call(queries, [above, below, facing], state)
    state = mid_call(queries, [near_other], state)
    far_above, far_below, state = lax.optimization_barrier((far_above, far_below, state))

    far_other = over_rep(jnp.concatenate([far_above, far_below]), perm=CORE_SWAP)
    state = mid_call(queries, [far_above, far_below], state)
    return reduce_rows(*last_call(spot, queries, [far_other], state, out_weight))


def solution(mesh):
    in_specs = (
        P("rep", "tp"),
        P("rep", "tp"),
        P("rep", "tp"),
        P("rep", None, None, "tp"),
        P(),
        P("rep", None),
        P("tp", None),
    )
    out_specs = P(("rep", "tp"), None)
    return jax.shard_map(body, mesh=mesh, in_specs=in_specs, out_specs=out_specs, check_vma=False)
```

profile of v0, /device:TPU:1, one launch (start us, length us, event | category | flops | bytes accessed | tf_op | source)
XLA Modules:
  0.0 100.9 jit_solution(5749786211621168718)
XLA Ops:
  0.0 3.2 %collective-permute-start.16 = (bf16[2,4096,128]{2,1,0:T(8,128)(2,1)}, bf16[2,4096,128]{2,1,0:T(8,128)(2,1)S(1)}, u32[]{:S(2)}, u32[]{:S(2)}) collective-permute-start(bf16[2,4096,128]{2,1,0:T(8,128)(2,1)} %bitcast.48), channel_id=1, source_target_pairs={{0,8},{8,0},{16,24},{24,16},{32,40},{40,32},{48,56},{56,48},{64,72... | collective-permute-start | bytes 6291464 | tf_op jit(solution)/shard_map/ppermute | solution.py:248
  4.1 3.1 %collective-permute-done.16 = bf16[2,4096,128]{2,1,0:T(8,128)(2,1)S(1)} collective-permute-done((bf16[2,4096,128]{2,1,0:T(8,128)(2,1)}, bf16[2,4096,128]{2,1,0:T(8,128)(2,1)S(1)}, u32[]{:S(2)}, u32[]{:S(2)}) %collective-permute-start.16) | collective-permute-done | bytes 2097184 | tf_op jit(solution)/shard_map/ppermute | solution.py:248
  7.2 1.6 %bitcast_select_fusion.4 = bf16[2,256,128]{2,1,0:T(8,128)(2,1)} fusion(bf16[2,4096,128]{2,1,0:T(8,128)(2,1)S(1)} %collective-permute-done.16, s32[]{:T(128)S(6)} %select_n.313, bf16[1,2,4096,128]{3,2,1,0:T(8,128)(2,1)} %param.14, pred[]{:T(512)S(6)} %eq.25), kind=kLoop, calls=%fused_computation.36 | loop fusion | flops 65536 | bytes 393221 | tf_op jit(solution)/shard_map/jit(_where)/select_n | solution.py:251
  8.8 2.2 %bitcast_select_fusion = (bf16[2,512,128]{2,1,0:T(8,128)(2,1)S(1)}, bf16[2,512,128]{2,1,0:T(8,128)(2,1)S(1)}, bf16[2,512,128]{2,1,0:T(8,128)(2,1)S(1)}, bf16[2,512,128]{2,1,0:T(8,128)(2,1)}) fusion(bf16[2,4096,128]{2,1,0:T(8,128)(2,1)S(1)} %collective-permute-done.16, s32[]{:T(128)S(6)} %select_n.309, bf16[1,2,4096,128]{3,2,1,0:T(8,128)(2,1)} %param.14, ...), kind=kLoop, calls=%fused_computation.28 | loop fusion | flops 524288 | bytes 3145745 | tf_op jit(solution)/shard_map/jit(_where)/select_n | solution.py:251
  11.0 14.3 %conditional.1 = (bf16[2,512,128]{2,1,0:T(8,128)(2,1)S(1)}) conditional(s32[]{:T(128)} %clamp.3, (s32[]{:T(128)}, bf16[2,512,128]{2,1,0:T(8,128)(2,1)}, bf16[2,512,128]{2,1,0:T(8,128)(2,1)S(1)}, bf16[2,512,128]{2,1,0:T(8,128)(2,1)S(1)}, bf16[2,512,128]{2,1,0:T(8,128)(2,1)S(1)}, ...), branch_computations={%region_0.1_spmd, %region_1.2_spmd, %region_2.3_spmd, %region_3.4_... | conditional | flops 1048581 | bytes 5112028 | solution.py:277
  14.5 10.6 %collective-permute-done.14 = bf16[2,512,128]{2,1,0:T(8,128)(2,1)S(1)} collective-permute-done((bf16[2,512,128]{2,1,0:T(8,128)(2,1)S(1)}, bf16[2,512,128]{2,1,0:T(8,128)(2,1)S(1)}, u32[]{:S(2)}, u32[]{:S(2)}) %collective-permute-start.14) | collective-permute-done | bytes 262176 | tf_op jit(solution)/shard_map/cond/branch_3_fun/ppermute | solution.py:271
  26.8 3.0 %collective-permute-start.18 = (bf16[2,256,128]{2,1,0:T(8,128)(2,1)S(1)}, bf16[2,256,128]{2,1,0:T(8,128)(2,1)S(1)}, u32[]{:S(2)}, u32[]{:S(2)}) collective-permute-start(bf16[2,256,128]{2,1,0:T(8,128)(2,1)S(1)} %dynamic-slice_select_fusion), channel_id=1, source_target_pairs={{0,128},{8,136},{16,144},{24,152},{32,160},{40,168},{48,176},{56,1... | collective-permute-start | bytes 393224 | tf_op jit(solution)/shard_map/ppermute | solution.py:283
  29.8 3.4 %collective-permute-done.18 = bf16[2,256,128]{2,1,0:T(8,128)(2,1)S(1)} collective-permute-done((bf16[2,256,128]{2,1,0:T(8,128)(2,1)S(1)}, bf16[2,256,128]{2,1,0:T(8,128)(2,1)S(1)}, u32[]{:S(2)}, u32[]{:S(2)}) %collective-permute-start.18) | collective-permute-done | bytes 131104 | tf_op jit(solution)/shard_map/ppermute | solution.py:283
  33.3 6.0 %collective-permute-start.19 = (bf16[1,2,256,128]{3,2,1,0:T(8,128)(2,1)S(1)}, bf16[1,2,256,128]{3,2,1,0:T(8,128)(2,1)S(1)}, u32[]{:S(2)}, u32[]{:S(2)}) collective-permute-start(bf16[1,2,256,128]{3,2,1,0:T(8,128)(2,1)S(1)} %select_bitcast_fusion.a0), channel_id=1, source_target_pairs={{0,112},{8,120},{16,0},{24,8},{32,16},{40,24},{48,32},{56,40},{64,... | collective-permute-start | bytes 393224 | tf_op jit(solution)/shard_map/ppermute | solution.py:287
  39.3 4.5 %collective-permute-start.21 = (bf16[1,2,256,128]{3,2,1,0:T(8,128)(2,1)S(1)}, bf16[1,2,256,128]{3,2,1,0:T(8,128)(2,1)S(1)}, u32[]{:S(2)}, u32[]{:S(2)}) collective-permute-start(bf16[1,2,256,128]{3,2,1,0:T(8,128)(2,1)S(1)} %select_bitcast_fusion.a0), channel_id=1, source_target_pairs={{0,64},{8,72},{16,80},{24,88},{32,96},{40,104},{48,112},{56,120},{... | collective-permute-start | bytes 393224 | tf_op jit(solution)/shard_map/ppermute | solution.py:289
  43.8 2.1 %attn_first.1 = (f32[8,256,128]{2,1,0:T(8,128)S(1)}, f32[8,256,256]{2,1,0:T(8,128)S(1)}) custom-call(s32[2]{0:T(128)S(1)} %bitcast.47, bf16[256,1024]{1,0:T(8,128)(2,1)S(1)} %copy-done, bf16[256,128]{1,0:T(8,128)(2,1)S(1)} %copy-done.1, bf16[256,128]{1,0:T(8,128)(2,1)S(1)} %copy-done.2, bf16[1,2,256,128]{3,2,1,0:T(8,128)(2,1)S(1)} %select_bitcast_fusion.a0), custom_call_target="tpu_custom_call" | custom-call | flops 536870912 | tf_op jit(solution)/shard_map/attn_first/pallas_call | solution.py:173
  45.9 4.2 %collective-permute-done.21.refs_2_ = bf16[1,2,256,128]{3,2,1,0:T(8,128)(2,1)S(1)} collective-permute-done((bf16[1,2,256,128]{3,2,1,0:T(8,128)(2,1)S(1)}, bf16[1,2,256,128]{3,2,1,0:T(8,128)(2,1)S(1)}, u32[]{:S(2)}, u32[]{:S(2)}) %collective-permute-start.21) | collective-permute-done | bytes 131104 | tf_op jit(solution)/shard_map/ppermute | solution.py:289
  50.2 3.7 %collective-permute-start.24 = (bf16[4,2,256,128]{3,2,1,0:T(8,128)(2,1)S(1)}, bf16[4,2,256,128]{3,2,1,0:T(8,128)(2,1)S(1)}, u32[]{:S(2)}, u32[]{:S(2)}) collective-permute-start(bf16[4,2,256,128]{3,2,1,0:T(8,128)(2,1)S(1)} %pad_maximum_fusion), channel_id=1, source_target_pairs={{0,8},{8,0},{16,24},{24,16},{32,40},{40,32},{48,56},{56,48},{64,72... | collective-permute-start | bytes 1572872 | tf_op jit(solution)/shard_map/ppermute | solution.py:295
  55.5 3.0 %attn_mid.3 = (f32[8,256,128]{2,1,0:T(8,128)S(1)}, f32[8,256,256]{2,1,0:T(8,128)S(1)}) custom-call(bf16[256,1024]{1,0:T(8,128)(2,1)S(1)} %copy-done, bf16[1,2,256,128]{3,2,1,0:T(8,128)(2,1)S(1)} %collective-permute-done.19.refs_0_, bf16[1,2,256,128]{3,2,1,0:T(8,128)(2,1)S(1)} %collective-permute-done.20.refs_1_, ...), custom_call_target="tpu_custom_call", output_to_operand_aliasing={{0}: (4, {}), {1}: (5, {})} | custom-call | flops 805306368 | tf_op jit(solution)/shard_map/attn_mid/pallas_call | solution.py:187
  58.5 3.9 %attn_mid.4 = (f32[8,256,128]{2,1,0:T(8,128)S(1)}, f32[8,256,256]{2,1,0:T(8,128)S(1)}) custom-call(bf16[256,1024]{1,0:T(8,128)(2,1)S(1)} %copy-done, bf16[4,2,256,128]{3,2,1,0:T(8,128)(2,1)S(1)} %collective-permute-done.24.refs_0_, f32[8,256,128]{2,1,0:T(8,128)S(1)} %get-tuple-element.116.refs_1_, ...), custom_call_target="tpu_custom_call", output_to_operand_aliasing={{0}: (2, {}), {1}: (3, {})} | custom-call | flops 1073741824 | tf_op jit(solution)/shard_map/attn_mid/pallas_call | solution.py:187
  64.6 3.8 %attn_mid.5 = (f32[8,256,128]{2,1,0:T(8,128)S(1)}, f32[8,256,256]{2,1,0:T(8,128)S(1)}) custom-call(bf16[256,1024]{1,0:T(8,128)(2,1)S(1)} %copy-done, bf16[2,2,256,128]{3,2,1,0:T(8,128)(2,1)S(1)} %collective-permute-done.22.refs_0_, bf16[2,2,256,128]{3,2,1,0:T(8,128)(2,1)S(1)} %collective-permute-done.23.refs_1_, ...), custom_call_target="tpu_custom_call", output_to_operand_aliasing={{0}: (3, {}), {1}: (4, {})} | custom-call | flops 1073741824 | tf_op jit(solution)/shard_map/attn_mid/pallas_call | solution.py:187
  68.4 5.9 %attn_last.1 = (bf16[2,32,2048]{2,1,0:T(8,128)(2,1)S(1)}, bf16[2,32,2048]{2,1,0:T(8,128)(2,1)S(1)}, bf16[2,32,2048]{2,1,0:T(8,128)(2,1)S(1)}, bf16[2,32,2048]{2,...) custom-call(s32[2]{0:T(128)S(1)} %pad_add_fusion.spot, ...), custom_call_target="tpu_custom_call" | custom-call | flops 3221225472 | tf_op jit(solution)/shard_map/attn_last/pallas_call | solution.py:204
  75.6 1.5 %collective-permute-start.27 = (bf16[2,32,2048]{2,1,0:T(8,128)(2,1)S(1)}, bf16[2,32,2048]{2,1,0:T(8,128)(2,1)S(1)}, u32[]{:S(2)}, u32[]{:S(2)}) collective-permute-start(bf16[2,32,2048]{2,1,0:T(8,128)(2,1)S(1)} %get-tuple-element.128), channel_id=1, source_target_pairs={{0,3},{1,0},{2,1},{3,2},{4,7},{5,4},{6,5},{7,6},{8,11},{9,8},{10,9... | collective-permute-start | bytes 786440 | tf_op jit(solution)/shard_map/ppermute | solution.py:225
  77.0 1.5 %collective-permute-start.28 = (bf16[2,32,2048]{2,1,0:T(8,128)(2,1)S(1)}, bf16[2,32,2048]{2,1,0:T(8,128)(2,1)S(1)}, u32[]{:S(2)}, u32[]{:S(2)}) collective-permute-start(bf16[2,32,2048]{2,1,0:T(8,128)(2,1)S(1)} %get-tuple-element.129), channel_id=1, source_target_pairs={{0,2},{1,3},{2,0},{3,1},{4,6},{5,7},{6,4},{7,5},{8,10},{9,11},{10,... | collective-permute-start | bytes 786440 | tf_op jit(solution)/shard_map/ppermute | solution.py:223
  79.9 3.6 %collective-permute-done.26 = bf16[2,32,2048]{2,1,0:T(8,128)(2,1)S(1)} collective-permute-done((bf16[2,32,2048]{2,1,0:T(8,128)(2,1)S(1)}, bf16[2,32,2048]{2,1,0:T(8,128)(2,1)S(1)}, u32[]{:S(2)}, u32[]{:S(2)}) %collective-permute-start.26) | collective-permute-done | bytes 262176 | tf_op jit(solution)/shard_map/ppermute | solution.py:224
  83.4 6.6 %collective-permute-done.28 = bf16[2,32,2048]{2,1,0:T(8,128)(2,1)S(1)} collective-permute-done((bf16[2,32,2048]{2,1,0:T(8,128)(2,1)S(1)}, bf16[2,32,2048]{2,1,0:T(8,128)(2,1)S(1)}, u32[]{:S(2)}, u32[]{:S(2)}) %collective-permute-start.28) | collective-permute-done | bytes 262176 | tf_op jit(solution)/shard_map/ppermute | solution.py:223
  92.4 2.1 %collective-permute-start.32 = (bf16[32,2048]{1,0:T(8,128)(2,1)S(1)}, bf16[32,2048]{1,0:T(8,128)(2,1)S(1)}, u32[]{:S(2)}, u32[]{:S(2)}) collective-permute-start(bf16[32,2048]{1,0:T(8,128)(2,1)S(1)} %get-tuple-element.140), channel_id=1, source_target_pairs={{0,3},{1,0},{2,1},{3,2},{4,7},{5,4},{6,5},{7,6},{8,11},{9,8},{10,9... | collective-permute-start | bytes 393224 | tf_op jit(solution)/shard_map/ppermute | solution.py:231
  94.5 2.3 %collective-permute-done.31 = bf16[32,2048]{1,0:T(8,128)(2,1)S(1)} collective-permute-done((bf16[32,2048]{1,0:T(8,128)(2,1)S(1)}, bf16[32,2048]{1,0:T(8,128)(2,1)S(1)}, u32[]{:S(2)}, u32[]{:S(2)}) %collective-permute-start.31) | collective-permute-done | bytes 131104 | tf_op jit(solution)/shard_map/ppermute | solution.py:230
  98.2 1.9 %collective-permute-done.33 = bf16[32,2048]{1,0:T(8,128)(2,1)S(1)} collective-permute-done((bf16[32,2048]{1,0:T(8,128)(2,1)S(1)}, bf16[32,2048]{1,0:T(8,128)(2,1)S(1)}, u32[]{:S(2)}, u32[]{:S(2)}) %collective-permute-start.33) | collective-permute-done | bytes 131104 | tf_op jit(solution)/shard_map/ppermute | solution.py:229
  (56 shorter events, 16.1 us)
Async XLA Ops:
  0.0 7.2 %collective-permute-start.16 = (bf16[2,4096,128]{2,1,0:T(8,128)(2,1)}, bf16[2,4096,128]{2,1,0:T(8,128)(2,1)S(1)}, u32[]{:S(2)}, u32[]{:S(2)}) collective-permute-start(bf16[2,4096,128]{2,1,0:T(8,128)(2,1)} %bitcast.48), channel_id=1, source_target_pairs={{0,8},{8,0},{16,24},{24,16},{32,40},{40,32},{48,56},{56,48},{64,72... | collective-permute-start | bytes 6291464 | tf_op jit(solution)/shard_map/ppermute | solution.py:248
  11.0 32.9 %copy-start.2 = (bf16[256,128]{1,0:T(8,128)(2,1)S(1)}, bf16[256,128]{1,0:T(8,128)(2,1)}, u32[]{:S(2)}) copy-start(bf16[256,128]{1,0:T(8,128)(2,1)} %cv.1) | copy-start | bytes 196612
  11.0 32.9 %copy-start.3 = (s32[1,2]{1,0:T(1,128)S(1)}, s32[1,2]{1,0:T(1,128)}, u32[]{:S(2)}) copy-start(s32[1,2]{1,0:T(1,128)} %param.16) | copy-start | bytes 28
  11.0 3.5 %collective-permute-start.12 = (bf16[2,512,128]{2,1,0:T(8,128)(2,1)}, bf16[2,512,128]{2,1,0:T(8,128)(2,1)S(1)}, u32[]{:S(2)}, u32[]{:S(2)}) collective-permute-start(bf16[2,512,128]{2,1,0:T(8,128)(2,1)} %get-tuple-element.78), channel_id=1, source_target_pairs={{48,64},{56,40},{112,0},{120,104},{176,192},{184,168},{240,128},{2... | collective-permute-start | bytes 786440 | tf_op jit(solution)/shard_map/cond/branch_3_fun/ppermute | solution.py:271
  11.8 2.7 %collective-permute-start.13 = (bf16[2,512,128]{2,1,0:T(8,128)(2,1)S(1)}, bf16[2,512,128]{2,1,0:T(8,128)(2,1)S(1)}, u32[]{:S(2)}, u32[]{:S(2)}) collective-permute-start(bf16[2,512,128]{2,1,0:T(8,128)(2,1)S(1)} %get-tuple-element.79), channel_id=1, source_target_pairs={{48,80},{56,24},{112,16},{120,88},{176,208},{184,152},{240,144},{2... | collective-permute-start | bytes 786440 | tf_op jit(solution)/shard_map/cond/branch_3_fun/ppermute | solution.py:271
  12.5 12.6 %collective-permute-start.14 = (bf16[2,512,128]{2,1,0:T(8,128)(2,1)S(1)}, bf16[2,512,128]{2,1,0:T(8,128)(2,1)S(1)}, u32[]{:S(2)}, u32[]{:S(2)}) collective-permute-start(bf16[2,512,128]{2,1,0:T(8,128)(2,1)S(1)} %get-tuple-element.80), channel_id=1, source_target_pairs={{48,96},{56,8},{112,32},{120,72},{176,224},{184,136},{240,160},{24... | collective-permute-start | bytes 786440 | tf_op jit(solution)/shard_map/cond/branch_3_fun/ppermute | solution.py:271
  13.8 0.7 collective-permute-start.15
  25.3 1.4 %collective-permute-start.17 = (bf16[2,256,128]{2,1,0:T(8,128)(2,1)S(1)}, bf16[2,256,128]{2,1,0:T(8,128)(2,1)S(1)}, u32[]{:S(2)}, u32[]{:S(2)}) collective-permute-start(bf16[2,256,128]{2,1,0:T(8,128)(2,1)S(1)} %constant_dynamic-slice_fusion), channel_id=1, source_target_pairs={{0,8},{8,0},{16,24},{24,16},{32,40},{40,32},{48,56},{56,48},{64,72... | collective-permute-start | bytes 393224 | tf_op jit(solution)/shard_map/ppermute | solution.py:281
  26.8 6.5 %collective-permute-start.18 = (bf16[2,256,128]{2,1,0:T(8,128)(2,1)S(1)}, bf16[2,256,128]{2,1,0:T(8,128)(2,1)S(1)}, u32[]{:S(2)}, u32[]{:S(2)}) collective-permute-start(bf16[2,256,128]{2,1,0:T(8,128)(2,1)S(1)} %dynamic-slice_select_fusion), channel_id=1, source_target_pairs={{0,128},{8,136},{16,144},{24,152},{32,160},{40,168},{48,176},{56,1... | collective-permute-start | bytes 393224 | tf_op jit(solution)/shard_map/ppermute | solution.py:283
  33.3 12.6 %collective-permute-start.19 = (bf16[1,2,256,128]{3,2,1,0:T(8,128)(2,1)S(1)}, bf16[1,2,256,128]{3,2,1,0:T(8,128)(2,1)S(1)}, u32[]{:S(2)}, u32[]{:S(2)}) collective-permute-start(bf16[1,2,256,128]{3,2,1,0:T(8,128)(2,1)S(1)} %select_bitcast_fusion.a0), channel_id=1, source_target_pairs={{0,112},{8,120},{16,0},{24,8},{32,16},{40,24},{48,32},{56,40},{64,... | collective-permute-start | bytes 393224 | tf_op jit(solution)/shard_map/ppermute | solution.py:287
  39.3 6.6 %collective-permute-start.20 = (bf16[1,2,256,128]{3,2,1,0:T(8,128)(2,1)S(1)}, bf16[1,2,256,128]{3,2,1,0:T(8,128)(2,1)S(1)}, u32[]{:S(2)}, u32[]{:S(2)}) collective-permute-start(bf16[1,2,256,128]{3,2,1,0:T(8,128)(2,1)S(1)} %select_bitcast_fusion.a0), channel_id=1, source_target_pairs={{0,16},{8,24},{16,32},{24,40},{32,48},{40,56},{48,64},{56,72},{64,... | collective-permute-start | bytes 393224 | tf_op jit(solution)/shard_map/ppermute | solution.py:288
  39.3 10.9 %collective-permute-start.21 = (bf16[1,2,256,128]{3,2,1,0:T(8,128)(2,1)S(1)}, bf16[1,2,256,128]{3,2,1,0:T(8,128)(2,1)S(1)}, u32[]{:S(2)}, u32[]{:S(2)}) collective-permute-start(bf16[1,2,256,128]{3,2,1,0:T(8,128)(2,1)S(1)} %select_bitcast_fusion.a0), channel_id=1, source_target_pairs={{0,64},{8,72},{16,80},{24,88},{32,96},{40,104},{48,112},{56,120},{... | collective-permute-start | bytes 393224 | tf_op jit(solution)/shard_map/ppermute | solution.py:289
  50.2 8.3 %collective-permute-start.24 = (bf16[4,2,256,128]{3,2,1,0:T(8,128)(2,1)S(1)}, bf16[4,2,256,128]{3,2,1,0:T(8,128)(2,1)S(1)}, u32[]{:S(2)}, u32[]{:S(2)}) collective-permute-start(bf16[4,2,256,128]{3,2,1,0:T(8,128)(2,1)S(1)} %pad_maximum_fusion), channel_id=1, source_target_pairs={{0,8},{8,0},{16,24},{24,16},{32,40},{40,32},{48,56},{56,48},{64,72... | collective-permute-start | bytes 1572872 | tf_op jit(solution)/shard_map/ppermute | solution.py:295
  53.9 8.5 %collective-permute-start.22 = (bf16[2,2,256,128]{3,2,1,0:T(8,128)(2,1)S(1)}, bf16[2,2,256,128]{3,2,1,0:T(8,128)(2,1)S(1)}, u32[]{:S(2)}, u32[]{:S(2)}) collective-permute-start(bf16[2,2,256,128]{3,2,1,0:T(8,128)(2,1)S(1)} %get-tuple-element.142), channel_id=1, source_target_pairs={{0,112},{8,120},{16,0},{24,8},{32,16},{40,24},{48,32},{56,40},{64,... | collective-permute-start | bytes 786440 | tf_op jit(solution)/shard_map/ppermute | solution.py:293
  54.2 9.0 %collective-permute-start.23 = (bf16[2,2,256,128]{3,2,1,0:T(8,128)(2,1)S(1)}, bf16[2,2,256,128]{3,2,1,0:T(8,128)(2,1)S(1)}, u32[]{:S(2)}, u32[]{:S(2)}) collective-permute-start(bf16[2,2,256,128]{3,2,1,0:T(8,128)(2,1)S(1)} %get-tuple-element.141), channel_id=1, source_target_pairs={{0,16},{8,24},{16,32},{24,40},{32,48},{40,56},{48,64},{56,72},{64,... | collective-permute-start | bytes 786440 | tf_op jit(solution)/shard_map/ppermute | solution.py:294
  63.2 5.1 %collective-permute-start.25 = (bf16[4,2,256,128]{3,2,1,0:T(8,128)(2,1)S(1)}, bf16[4,2,256,128]{3,2,1,0:T(8,128)(2,1)S(1)}, u32[]{:S(2)}, u32[]{:S(2)}) collective-permute-start(bf16[4,2,256,128]{3,2,1,0:T(8,128)(2,1)S(1)} %pad_maximum_fusion.1), channel_id=1, source_target_pairs={{0,8},{8,0},{16,24},{24,16},{32,40},{40,32},{48,56},{56,48},{64,72... | collective-permute-start | bytes 1572872 | tf_op jit(solution)/shard_map/ppermute | solution.py:300
  74.3 9.1 %collective-permute-start.26 = (bf16[2,32,2048]{2,1,0:T(8,128)(2,1)S(1)}, bf16[2,32,2048]{2,1,0:T(8,128)(2,1)S(1)}, u32[]{:S(2)}, u32[]{:S(2)}) collective-permute-start(bf16[2,32,2048]{2,1,0:T(8,128)(2,1)S(1)} %get-tuple-element.127), channel_id=1, source_target_pairs={{0,1},{1,2},{2,3},{3,0},{4,5},{5,6},{6,7},{7,4},{8,9},{9,10},{10,1... | collective-permute-start | bytes 786440 | tf_op jit(solution)/shard_map/ppermute | solution.py:224
  75.6 7.9 %collective-permute-start.27 = (bf16[2,32,2048]{2,1,0:T(8,128)(2,1)S(1)}, bf16[2,32,2048]{2,1,0:T(8,128)(2,1)S(1)}, u32[]{:S(2)}, u32[]{:S(2)}) collective-permute-start(bf16[2,32,2048]{2,1,0:T(8,128)(2,1)S(1)} %get-tuple-element.128), channel_id=1, source_target_pairs={{0,3},{1,0},{2,1},{3,2},{4,7},{5,4},{6,5},{7,6},{8,11},{9,8},{10,9... | collective-permute-start | bytes 786440 | tf_op jit(solution)/shard_map/ppermute | solution.py:225
  77.0 13.0 %collective-permute-start.28 = (bf16[2,32,2048]{2,1,0:T(8,128)(2,1)S(1)}, bf16[2,32,2048]{2,1,0:T(8,128)(2,1)S(1)}, u32[]{:S(2)}, u32[]{:S(2)}) collective-permute-start(bf16[2,32,2048]{2,1,0:T(8,128)(2,1)S(1)} %get-tuple-element.129), channel_id=1, source_target_pairs={{0,2},{1,3},{2,0},{3,1},{4,6},{5,7},{6,4},{7,5},{8,10},{9,11},{10,... | collective-permute-start | bytes 786440 | tf_op jit(solution)/shard_map/ppermute | solution.py:223
  78.6 13.0 %collective-permute-start.30 = (bf16[4,32,2048]{2,1,0:T(8,128)(2,1)S(1)}, bf16[4,32,2048]{2,1,0:T(8,128)(2,1)S(1)}, u32[]{:S(2)}, u32[]{:S(2)}) collective-permute-start(bf16[4,32,2048]{2,1,0:T(8,128)(2,1)S(1)} %get-tuple-element.131), channel_id=1, source_target_pairs={{0,4},{1,5},{2,6},{3,7},{4,0},{5,1},{6,2},{7,3},{8,12},{9,13},{10,... | collective-permute-start | bytes 1572872 | tf_op jit(solution)/shard_map/ppermute | solution.py:222
  90.2 4.3 %collective-permute-start.29 = (bf16[32,2048]{1,0:T(8,128)(2,1)S(1)}, bf16[32,2048]{1,0:T(8,128)(2,1)S(1)}, u32[]{:S(2)}, u32[]{:S(2)}) collective-permute-start(bf16[32,2048]{1,0:T(8,128)(2,1)S(1)} %fusion.14), channel_id=1, source_target_pairs={{0,4},{1,5},{2,6},{3,7},{4,0},{5,1},{6,2},{7,3},{8,12},{9,13},{10,... | collective-permute-start | bytes 393224 | tf_op jit(solution)/shard_map/ppermute | solution.py:232
  91.7 5.1 %collective-permute-start.31 = (bf16[32,2048]{1,0:T(8,128)(2,1)S(1)}, bf16[32,2048]{1,0:T(8,128)(2,1)S(1)}, u32[]{:S(2)}, u32[]{:S(2)}) collective-permute-start(bf16[32,2048]{1,0:T(8,128)(2,1)S(1)} %get-tuple-element.138), channel_id=1, source_target_pairs={{0,1},{1,2},{2,3},{3,0},{4,5},{5,6},{6,7},{7,4},{8,9},{9,10},{10,1... | collective-permute-start | bytes 393224 | tf_op jit(solution)/shard_map/ppermute | solution.py:230
  92.4 5.8 %collective-permute-start.32 = (bf16[32,2048]{1,0:T(8,128)(2,1)S(1)}, bf16[32,2048]{1,0:T(8,128)(2,1)S(1)}, u32[]{:S(2)}, u32[]{:S(2)}) collective-permute-start(bf16[32,2048]{1,0:T(8,128)(2,1)S(1)} %get-tuple-element.140), channel_id=1, source_target_pairs={{0,3},{1,0},{2,1},{3,2},{4,7},{5,4},{6,5},{7,6},{8,11},{9,8},{10,9... | collective-permute-start | bytes 393224 | tf_op jit(solution)/shard_map/ppermute | solution.py:231
  94.5 5.6 %collective-permute-start.33 = (bf16[32,2048]{1,0:T(8,128)(2,1)S(1)}, bf16[32,2048]{1,0:T(8,128)(2,1)S(1)}, u32[]{:S(2)}, u32[]{:S(2)}) collective-permute-start(bf16[32,2048]{1,0:T(8,128)(2,1)S(1)} %get-tuple-element.139), channel_id=1, source_target_pairs={{0,2},{1,3},{2,0},{3,1},{4,6},{5,7},{6,4},{7,5},{8,10},{9,11},{10,... | collective-permute-start | bytes 393224 | tf_op jit(solution)/shard_map/ppermute | solution.py:229
  (4 other events, 93.7 us)
where the time goes:
time: 102 us; the launch traced here: 101 us
  waiting for transfers between devices  39.2 us (38%)
  starting transfers between devices  36.5 us (36%)
  Pallas kernels  18.6 us (18%)
  other arithmetic  5.31 us (5%)
  between operations  1.07 us (1%)
    pallas_call x3, Pallas kernels, mid_call(): pl.pallas_call(functools.partial(mid_kernel, n), out_shape=state_shapes(r...  10.7 us
    ppermute x4, waiting for transfers between devices, send(): got[d] = over_rep(parts[d - 1], perm=pairs)  10.6 us
    ppermute x1, waiting for transfers between devices, reduce_rows(): r2 = over_tp(x2, perm=x_shift(2))  6.6 us
    ppermute x1, starting transfers between devices, body(): above = over_rep(a0, perm=z_shift(-1))  5.99 us
    pallas_call x1, Pallas kernels, last_call(): pl.pallas_call(functools.partial(last_kernel, n), out_shape=outs, in_spec...  5.9 us
    ppermute x1, starting transfers between devices, body(): facing = over_rep(a0, perm=z_shift(4))  4.53 us
    ppermute x1, waiting for transfers between devices, body(): facing = over_rep(a0, perm=z_shift(4))  4.23 us
    select_n x2, other arithmetic, body(): jnp.where(mine, lax.dynamic_slice_in_dim(prefix, start, size, 1), lax.dyn...  3.76 us
  transfers between devices with their start and end apart: 22, of which 11 were waited for; matrix products, arithmetic and copies ran while one was open for 0% of the time, Pallas kernels for 13%

commit v1 on v0

--- a/solution.py
+++ b/solution.py
@@ -74,13 +74,13 @@
 UNROLL = 8
 
 
-def each_head(f):
+def each_head(f, unroll=UNROLL):
     def step(i, carry):
-        for j in range(UNROLL):
-            f(i * UNROLL + j)
+        for j in range(unroll):
+            f(i * unroll + j)
         return carry
 
-    lax.fori_loop(0, HEADS // UNROLL, step, 0)
+    lax.fori_loop(0, HEADS // unroll, step, 0)
 
 
 def head_cols(h):
@@ -100,7 +100,7 @@
             q, [ck[...]] + keys, [cv[...]] + values, [mask] + [None] * len(keys), None, None
         )
 
-    each_head(head)
+    each_head(head, 4)
 
 
 def mid_kernel(n, q_ref, *refs):
@@ -117,8 +117,12 @@
 W_BLOCK = 512
 
 
+def product(rel, w, c):
+    return jnp.dot(rel, w[:, pl.ds(c, W_BLOCK)], preferred_element_type=jnp.float32).astype(jnp.bfloat16)
+
+
 def last_kernel(n, spot, q_ref, *refs):
-    m_in, acc_in, w, own_a, x1, x2, x3, own_b, yb, ctx = refs[n:]
+    m_in, acc_in, w, rel_out, own_b, yb, ctx = refs[n:]
 
     def head(h):
         keys, values = pieces(refs[:n])
@@ -126,28 +130,32 @@
         _, acc = absorb(q, keys, values, [None] * len(keys), m_in[h], acc_in[h])
         ctx[:, head_cols(h)] = (acc[:, :HD] / acc[:, HD:]).astype(jnp.bfloat16)
 
-    each_head(head)
-
-    tile = own_a.shape[1]
-    half = own_a.shape[2]
+    each_head(head, 4)
+
+    tile = own_b.shape[1]
+    half = own_b.shape[2]
     tp_of = [((spot[0] + dy) % 2) * 4 + (spot[1] + dx) % 4 for dy in range(2) for dx in range(4)]
     rel = jnp.concatenate([ctx[pl.ds(pl.multiple_of(t * tile, tile), tile)] for t in tp_of], axis=0)
-
-    def product(c):
-        return jnp.dot(rel, w[:, pl.ds(c, W_BLOCK)], preferred_element_type=jnp.float32).astype(jnp.bfloat16)
-
+    rel_out[...] = rel
     for c in range(0, half, W_BLOCK):
-        y = product(half + c)
+        y = product(rel, w, half + c)
         for dy, ref in enumerate((own_b, yb)):
             for dx in range(4):
                 ref[dx, :, pl.ds(c, W_BLOCK)] = y[(dy * 4 + dx) * tile : (dy * 4 + dx + 1) * tile]
-        y = product(c)
+
+
+def left_kernel(rel_ref, w, own_a, x1, x2, x3):
+    tile = own_a.shape[1]
+    rel = rel_ref[...]
+    for c in range(0, own_a.shape[2], W_BLOCK):
+        y = product(rel, w, c)
         for dx, ref in enumerate((own_a, x1, x2, x3)):
             for dy in range(2):
                 ref[dy, :, pl.ds(c, W_BLOCK)] = y[(dy * 4 + dx) * tile : (dy * 4 + dx + 1) * tile]
 
 
 VM = pl.BlockSpec(memory_space=pltpu.VMEM)
+ANY = pl.BlockSpec(memory_space=pl.ANY)
 SM = pl.BlockSpec(memory_space=pltpu.SMEM)
 
 
@@ -166,6 +174,51 @@
 
 def key_count(kvs):
     return sum(a.shape[0] for a in kvs) * PIECE
+
+
+def moves(pairs, sem):
+    copies = [pltpu.make_async_copy(source, target, sem.at[i]) for i, (source, target) in enumerate(pairs)]
+    for copy in copies:
+        copy.start()
+    for copy in copies:
+        copy.wait()
+
+
+def windows(at, source):
+    z, c = at[1], at[2]
+    up = 1 - 2 * c
+    spots = [(lax.rem(z + up * d + 8, 8) * 2 * PIECE, 2 * PIECE) for d in range(4)]
+    spots.append((lax.rem(z + 4, 8) * 2 * PIECE + c * PIECE, PIECE))
+    return [source.at[:, pl.ds(pl.multiple_of(start, PIECE), size)] for start, size in spots]
+
+
+def cut_kernel(at, prefix, *refs):
+    moves(zip(windows(at, prefix), refs[:-1]), refs[-1])
+
+
+def choose_kernel(at, partner, *refs):
+    mine, outs, sem = refs[:5], refs[5:10], refs[10]
+
+    @pl.when(at[0] == 1)
+    def _():
+        moves(zip(mine, outs), sem)
+
+    @pl.when(at[0] == 0)
+    def _():
+        moves(zip(windows(at, partner), outs), sem)
+
+
+def cut_call(kernel, at, source, *mine):
+    part = lambda size: jax.ShapeDtypeStruct((2, size, HD), jnp.bfloat16)
+    return pl.pallas_call(
+        kernel,
+        out_shape=(part(2 * PIECE),) * 4 + (part(PIECE),),
+        in_specs=[SM] + [ANY] * (1 + len(mine)),
+        out_specs=(VM,) * 5,
+        scratch_shapes=[pltpu.SemaphoreType.DMA((5,))],
+        compiler_params=pltpu.CompilerParams(vmem_limit_bytes=4 << 20),
+        cost_estimate=pl.CostEstimate(flops=1 << 28, transcendentals=0, bytes_accessed=0),
+    )(at, source, *mine)
 
 
 def first_call(lens, q, ck, cv, a0):
@@ -200,35 +253,50 @@
     n = len(kvs)
     rows = q.shape[0]
     part = lambda k: jax.ShapeDtypeStruct((k, rows // 8, w.shape[1] // 2), jnp.bfloat16)
-    outs = (part(2), part(2), part(2), part(2), part(4), part(4))
+    outs = (jax.ShapeDtypeStruct((rows, w.shape[0]), jnp.bfloat16), part(4), part(4))
     return pl.pallas_call(
         functools.partial(last_kernel, n),
         out_shape=outs,
         in_specs=[SM] + [VM] * (n + 4),
         out_specs=(VM,) * len(outs),
         scratch_shapes=[pltpu.VMEM((rows, w.shape[0]), jnp.bfloat16)],
-        cost_estimate=cost(rows, key_count(kvs), 2 * rows * w.shape[0] * w.shape[1]),
+        cost_estimate=cost(rows, key_count(kvs), rows * w.shape[0] * w.shape[1]),
         compiler_params=pltpu.CompilerParams(vmem_limit_bytes=12 << 20),
         name="attn_last",
     )(spot, q, *kvs, *state, w)
 
 
+def left_call(rel, w):
+    rows = rel.shape[0]
+    part = jax.ShapeDtypeStruct((2, rows // 8, w.shape[1] // 2), jnp.bfloat16)
+    return pl.pallas_call(
+        left_kernel,
+        out_shape=(part,) * 4,
+        in_specs=[VM] * 2,
+        out_specs=(VM,) * 4,
+        cost_estimate=pl.CostEstimate(flops=rows * w.shape[0] * w.shape[1], transcendentals=0, bytes_accessed=0),
+        compiler_params=pltpu.CompilerParams(vmem_limit_bytes=12 << 20),
+        name="project_left",
+    )(rel, w)
+
+
 def f32(a):
     return a.astype(jnp.float32)
 
 
-def reduce_rows(own_a, x1, x2, x3, own_b, yb):
+def reduce_rows(rel, own_b, yb, w):
     over_tp = functools.partial(lax.ppermute, axis_name="tp")
     ry = over_tp(yb, perm=YLO_SWAP)
+    own_a, x1, x2, x3 = left_call(rel, w)
     r2 = over_tp(x2, perm=x_shift(2))
     r1 = over_tp(x1, perm=x_shift(1))
     r3 = over_tp(x3, perm=x_shift(-1))
-    s = f32(own_a) + f32(r1) + f32(r3) + f32(r2)
     u = f32(own_b) + f32(ry)
     ub = u.astype(jnp.bfloat16)
-    t2 = over_tp(ub[2], perm=x_shift(2))
     t1 = over_tp(ub[1], perm=x_shift(1))
     t3 = over_tp(ub[3], perm=x_shift(-1))
+    t2 = over_tp(ub[2], perm=x_shift(2))
+    s = f32(own_a) + f32(r1) + f32(r3) + f32(r2)
     ty = over_tp(s[1].astype(jnp.bfloat16), perm=YLO_SWAP)
     left = s[0] + f32(ty)
     right = u[0] + f32(t1) + f32(t3) + f32(t2)
@@ -244,28 +312,25 @@
     root_yh, root_z, root_c = root // 16, (root // 2) % 8, root % 2
     over_rep = functools.partial(lax.ppermute, axis_name="rep")
 
-    prefix = prefix_kv[0]
-    partner = over_rep(prefix, perm=CORE_SWAP)
-    mine = my_c == root_c
-    up = 1 - 2 * my_c
-    pick = lambda start, size: jnp.where(
-        mine,
-        lax.dynamic_slice_in_dim(prefix, start, size, 1),
-        lax.dynamic_slice_in_dim(partner, start, size, 1),
-    )
-    whole = lambda d: pick(((my_z + up * d) % 8) * 2 * PIECE, 2 * PIECE)
-    opposite = pick(((my_z + 4) % 8) * 2 * PIECE + my_c * PIECE, PIECE)
+    cut_at = jnp.stack([my_c == root_c, my_z, my_c]).astype(jnp.int32)
     steps = (my_z - root_z) % 8
     steps = jnp.where(my_c == 0, steps, (8 - steps) % 8)
+    prefix, cut_at, spot, steps, root_z, root_yh, my_c, my_yh = lax.optimization_barrier(
+        (prefix_kv[0], cut_at, spot, steps, root_z, root_yh, my_c, my_yh)
+    )
+    partner = over_rep(prefix, perm=CORE_SWAP)
+    parts = cut_call(cut_kernel, cut_at, prefix)
+    own, *outgoing = cut_call(choose_kernel, cut_at, partner, *parts)
 
     def branch(b):
         def send(steps, own, *parts):
             got = {}
             for d in (3, 4, 2, 1):
+                roots = {1: range(b % 2, 8, 2), 2: (b % 4, b % 4 + 4)}.get(d, (b,))
                 pairs = [
                     (rep_id(y, z, c), rep_id(y, z + (1 - 2 * c) * d, c))
                     for y in range(2)
-                    for z in (b, b + 4)
+                    for z in roots
                     for c in range(2)
                 ]
                 got[d] = over_rep(parts[d - 1], perm=pairs)
@@ -274,19 +339,16 @@
 
         return send
 
-    slot = lax.switch(
-        root_z % 4, [branch(b) for b in range(4)], steps, whole(0), whole(1), whole(2), whole(3), opposite
-    )
+    slot = lax.switch(root_z, [branch(b) for b in range(8)], steps, own, *outgoing)
     half_of = lambda a, c: lax.dynamic_slice_in_dim(a, c * PIECE, PIECE, 1)
     from_partner = over_rep(half_of(slot, 1 - my_c), perm=CORE_SWAP)
     piece = jnp.where(steps <= 4, half_of(slot, my_c), from_partner)
     across = over_rep(piece, perm=YHI_SWAP)
     a0 = jnp.where(my_yh == root_yh, piece, across)[None]
-    a0, spot = lax.optimization_barrier((a0, spot))
-
+
+    facing = over_rep(a0, perm=z_shift(4))
     above = over_rep(a0, perm=z_shift(-1))
     below = over_rep(a0, perm=z_shift(1))
-    facing = over_rep(a0, perm=z_shift(4))
     state = first_call(lengths[0], queries, cand_keys, cand_values, a0)
     above, below, facing, state = lax.optimization_barrier((above, below, facing, state))
 
@@ -299,7 +361,7 @@
 
     far_other = over_rep(jnp.concatenate([far_above, far_below]), perm=CORE_SWAP)
     state = mid_call(queries, [far_above, far_below], state)
-    return reduce_rows(*last_call(spot, queries, [far_other], state, out_weight))
+    return reduce_rows(*last_call(spot, queries, [far_other], state, out_weight), out_weight)
 
 
 def solution(mesh):

time: 102 us -> 102 us (level)
  waiting for transfers between devices: 39.2 us -> 30.3 us
  starting transfers between devices: 36.5 us -> 44.1 us
  other arithmetic: 5.31 us -> 1.62 us
  Pallas kernels: 18.6 us -> 21.3 us
  local copies, waits for them, and re-layouts: 0.09 us -> 1.69 us
    ppermute x4, waiting for transfers between devices: 10.6 us -> 4.05 us  [send(): got[d] = over_rep(parts[d - 1], perm=pairs)]
    select_n x2 -> x0, other arithmetic: 3.76 us -> none  [body(): jnp.where(mine, lax.dynamic_slice_in_dim(prefix, start, size, 1), lax.dyn...]
    ppermute x1, starting transfers between devices: 5.99 us -> 9.18 us  [body(): above = over_rep(a0, perm=z_shift(-1))]
    pallas_call x0 -> x3, Pallas kernels: none -> 2.83 us  [the longest x2 1.55 us: cut_call(): pl.pallas_call(kernel, out_shape=(part(2 * PIECE),) * 4 + (part(PIECE),),...]
    ppermute x1, starting transfers between devices: 0.09 us -> 2.89 us  [body(): from_partner = over_rep(half_of(slot, 1 - my_c), perm=CORE_SWAP)]
    unnamed x12 -> x14, local copies, waits for them, and re-layouts: 0.03 us -> 1.63 us
    ppermute x1, starting transfers between devices: 4.53 us -> 6.07 us  [body(): facing = over_rep(a0, perm=z_shift(4))]
    ppermute x1, waiting for transfers between devices: 3.15 us -> 1.63 us  [body(): partner = over_rep(prefix, perm=CORE_SWAP)]
  transfers between devices with their start and end apart: 22 -> 22, of which waited for: 11 -> 11; matrix products, arithmetic and copies ran while one was open for 0% -> 0% of each run, Pallas kernels for 13% -> 14%
where the time goes in v1:
time: 102 us; the launch traced here: 100 us
  starting transfers between devices  44.1 us (43%)
  waiting for transfers between devices  30.3 us (30%)
  Pallas kernels  21.3 us (21%)
  local copies, waits for them, and re-layouts  1.69 us (2%)
  other arithmetic  1.62 us (2%)
  between operations  1.06 us (1%)
    pallas_call x3, Pallas kernels, mid_call(): pl.pallas_call(functools.partial(mid_kernel, n), out_shape=state_shapes(r...  10.7 us
    ppermute x1, starting transfers between devices, body(): above = over_rep(a0, perm=z_shift(-1))  9.18 us
    ppermute x1, waiting for transfers between devices, reduce_rows(): r2 = over_tp(x2, perm=x_shift(2))  6.6 us
    ppermute x1, starting transfers between devices, body(): facing = over_rep(a0, perm=z_shift(4))  6.07 us
    pallas_call x1, Pallas kernels, last_call(): pl.pallas_call(functools.partial(last_kernel, n), out_shape=outs, in_spec...  5.32 us
    ppermute x4, waiting for transfers between devices, send(): got[d] = over_rep(parts[d - 1], perm=pairs)  4.05 us
    ppermute x1, starting transfers between devices, body(): over_rep(jnp.concatenate([a0, above, below, facing]), perm=CORE_SWAP)  3.86 us
    ppermute x1, waiting for transfers between devices, body(): facing = over_rep(a0, perm=z_shift(4))  3.76 us
  transfers between devices with their start and end apart: 22, of which 11 were waited for; matrix products, arithmetic and copies ran while one was open for 0% of the time, Pallas kernels for 14%

profile of v1, /device:TPU:1, one launch (start us, length us, event | category | flops | bytes accessed | tf_op | source)
XLA Modules:
  0.0 100.2 jit_solution(11272654493721324715)
XLA Ops:
  1.0 3.2 %collective-permute-start.32 = (bf16[2,4096,128]{2,1,0:T(8,128)(2,1)}, bf16[2,4096,128]{2,1,0:T(8,128)(2,1)S(1)}, u32[]{:S(2)}, u32[]{:S(2)}) collective-permute-start(bf16[2,4096,128]{2,1,0:T(8,128)(2,1)} %bitcast.40), channel_id=1, source_target_pairs={{0,8},{8,0},{16,24},{24,16},{32,40},{40,32},{48,56},{56,48},{64,72... | collective-permute-start | bytes 6291464 | tf_op jit(solution)/shard_map/ppermute | solution.py:321
  4.2 1.6 %copy-done.1 = bf16[1,2,4096,128]{3,2,1,0:T(8,128)(2,1)S(1)} copy-done((bf16[1,2,4096,128]{3,2,1,0:T(8,128)(2,1)S(1)}, bf16[1,2,4096,128]{3,2,1,0:T(8,128)(2,1)}, u32[]{:S(2)}) %copy-start.1) | copy-done | bytes 2097176
  6.6 1.6 %collective-permute-done.32.partner = bf16[2,4096,128]{2,1,0:T(8,128)(2,1)S(1)} collective-permute-done((bf16[2,4096,128]{2,1,0:T(8,128)(2,1)}, bf16[2,4096,128]{2,1,0:T(8,128)(2,1)S(1)}, u32[]{:S(2)}, u32[]{:S(2)}) %collective-permute-start.32) | collective-permute-done | bytes 2097184 | tf_op jit(solution)/shard_map/ppermute | solution.py:321
  9.0 7.8 %conditional.1 = (bf16[2,512,128]{2,1,0:T(8,128)(2,1)S(1)}) conditional(s32[]{:T(128)} %clamp.3, (s32[]{:T(128)}, bf16[2,512,128]{2,1,0:T(8,128)(2,1)S(1)}, bf16[2,512,128]{2,1,0:T(8,128)(2,1)S(1)}, bf16[2,512,128]{2,1,0:T(8,128)(2,1)S(1)}, bf16[2,512,128]{2,1,0:T(8,128)(2,1)S(1)}, ...), branch_computations={%region_0.1_spmd, %region_1.2_spmd, %region_2.3_spmd, %region_3.4_... | conditional | flops 1048581 | bytes 5112028 | solution.py:342
  12.6 4.0 %collective-permute-done.28 = bf16[2,512,128]{2,1,0:T(8,128)(2,1)S(1)} collective-permute-done((bf16[2,512,128]{2,1,0:T(8,128)(2,1)S(1)}, bf16[2,512,128]{2,1,0:T(8,128)(2,1)S(1)}, u32[]{:S(2)}, u32[]{:S(2)}) %collective-permute-start.28) | collective-permute-done | bytes 262176 | tf_op jit(solution)/shard_map/cond/branch_7_fun/ppermute | solution.py:336
  16.8 2.9 %collective-permute-start.33 = (bf16[2,256,128]{2,1,0:T(8,128)(2,1)S(1)}, bf16[2,256,128]{2,1,0:T(8,128)(2,1)S(1)}, u32[]{:S(2)}, u32[]{:S(2)}) collective-permute-start(bf16[2,256,128]{2,1,0:T(8,128)(2,1)S(1)} %constant_dynamic-slice_fusion), channel_id=1, source_target_pairs={{0,8},{8,0},{16,24},{24,16},{32,40},{40,32},{48,56},{56,48},{64,72... | collective-permute-start | bytes 393224 | tf_op jit(solution)/shard_map/ppermute | solution.py:344
  20.7 3.0 %collective-permute-start.34 = (bf16[2,256,128]{2,1,0:T(8,128)(2,1)S(1)}, bf16[2,256,128]{2,1,0:T(8,128)(2,1)S(1)}, u32[]{:S(2)}, u32[]{:S(2)}) collective-permute-start(bf16[2,256,128]{2,1,0:T(8,128)(2,1)S(1)} %dynamic-slice_select_fusion), channel_id=1, source_target_pairs={{0,128},{8,136},{16,144},{24,152},{32,160},{40,168},{48,176},{56,1... | collective-permute-start | bytes 393224 | tf_op jit(solution)/shard_map/ppermute | solution.py:346
  23.7 3.3 %collective-permute-done.34 = bf16[2,256,128]{2,1,0:T(8,128)(2,1)S(1)} collective-permute-done((bf16[2,256,128]{2,1,0:T(8,128)(2,1)S(1)}, bf16[2,256,128]{2,1,0:T(8,128)(2,1)S(1)}, u32[]{:S(2)}, u32[]{:S(2)}) %collective-permute-start.34) | collective-permute-done | bytes 131104 | tf_op jit(solution)/shard_map/ppermute | solution.py:346
  27.0 9.2 %collective-permute-start.35 = (bf16[1,2,256,128]{3,2,1,0:T(8,128)(2,1)S(1)}, bf16[1,2,256,128]{3,2,1,0:T(8,128)(2,1)S(1)}, u32[]{:S(2)}, u32[]{:S(2)}) collective-permute-start(bf16[1,2,256,128]{3,2,1,0:T(8,128)(2,1)S(1)} %select_bitcast_fusion.a0), channel_id=1, source_target_pairs={{0,112},{8,120},{16,0},{24,8},{32,16},{40,24},{48,32},{56,40},{64,... | collective-permute-start | bytes 393224 | tf_op jit(solution)/shard_map/ppermute | solution.py:350
  36.2 6.1 %collective-permute-start.37 = (bf16[1,2,256,128]{3,2,1,0:T(8,128)(2,1)S(1)}, bf16[1,2,256,128]{3,2,1,0:T(8,128)(2,1)S(1)}, u32[]{:S(2)}, u32[]{:S(2)}) collective-permute-start(bf16[1,2,256,128]{3,2,1,0:T(8,128)(2,1)S(1)} %select_bitcast_fusion.a0), channel_id=1, source_target_pairs={{0,64},{8,72},{16,80},{24,88},{32,96},{40,104},{48,112},{56,120},{... | collective-permute-start | bytes 393224 | tf_op jit(solution)/shard_map/ppermute | solution.py:349
  42.3 2.5 %attn_first.1 = (f32[8,256,128]{2,1,0:T(8,128)S(1)}, f32[8,256,256]{2,1,0:T(8,128)S(1)}) custom-call(s32[2]{0:T(128)S(1)} %bitcast.42, bf16[256,1024]{1,0:T(8,128)(2,1)S(1)} %copy-done, bf16[256,128]{1,0:T(8,128)(2,1)S(1)} %copy-done.2, bf16[256,128]{1,0:T(8,128)(2,1)S(1)} %copy-done.3, bf16[1,2,256,128]{3,2,1,0:T(8,128)(2,1)S(1)} %select_bitcast_fusion.a0), custom_call_target="tpu_custom_call" | custom-call | flops 536870912 | tf_op jit(solution)/shard_map/attn_first/pallas_call | solution.py:226
  44.8 3.8 %collective-permute-done.37.refs_2_ = bf16[1,2,256,128]{3,2,1,0:T(8,128)(2,1)S(1)} collective-permute-done((bf16[1,2,256,128]{3,2,1,0:T(8,128)(2,1)S(1)}, bf16[1,2,256,128]{3,2,1,0:T(8,128)(2,1)S(1)}, u32[]{:S(2)}, u32[]{:S(2)}) %collective-permute-start.37) | collective-permute-done | bytes 131104 | tf_op jit(solution)/shard_map/ppermute | solution.py:349
  48.7 3.9 %collective-permute-start.40 = (bf16[4,2,256,128]{3,2,1,0:T(8,128)(2,1)S(1)}, bf16[4,2,256,128]{3,2,1,0:T(8,128)(2,1)S(1)}, u32[]{:S(2)}, u32[]{:S(2)}) collective-permute-start(bf16[4,2,256,128]{3,2,1,0:T(8,128)(2,1)S(1)} %pad_maximum_fusion), channel_id=1, source_target_pairs={{0,8},{8,0},{16,24},{24,16},{32,40},{40,32},{48,56},{56,48},{64,72... | collective-permute-start | bytes 1572872 | tf_op jit(solution)/shard_map/ppermute | solution.py:357
  54.1 3.1 %attn_mid.3 = (f32[8,256,128]{2,1,0:T(8,128)S(1)}, f32[8,256,256]{2,1,0:T(8,128)S(1)}) custom-call(bf16[256,1024]{1,0:T(8,128)(2,1)S(1)} %copy-done, bf16[1,2,256,128]{3,2,1,0:T(8,128)(2,1)S(1)} %collective-permute-done.35.refs_0_, bf16[1,2,256,128]{3,2,1,0:T(8,128)(2,1)S(1)} %collective-permute-done.36.refs_1_, ...), custom_call_target="tpu_custom_call", output_to_operand_aliasing={{0}: (4, {}), {1}: (5, {})} | custom-call | flops 805306368 | tf_op jit(solution)/shard_map/attn_mid/pallas_call | solution.py:240
  57.2 3.9 %attn_mid.4 = (f32[8,256,128]{2,1,0:T(8,128)S(1)}, f32[8,256,256]{2,1,0:T(8,128)S(1)}) custom-call(bf16[256,1024]{1,0:T(8,128)(2,1)S(1)} %copy-done, bf16[4,2,256,128]{3,2,1,0:T(8,128)(2,1)S(1)} %collective-permute-done.40.refs_0_, f32[8,256,128]{2,1,0:T(8,128)S(1)} %get-tuple-element.225.refs_1_, ...), custom_call_target="tpu_custom_call", output_to_operand_aliasing={{0}: (2, {}), {1}: (3, {})} | custom-call | flops 1073741824 | tf_op jit(solution)/shard_map/attn_mid/pallas_call | solution.py:240
  63.2 3.8 %attn_mid.5 = (f32[8,256,128]{2,1,0:T(8,128)S(1)}, f32[8,256,256]{2,1,0:T(8,128)S(1)}) custom-call(bf16[256,1024]{1,0:T(8,128)(2,1)S(1)} %copy-done, bf16[2,2,256,128]{3,2,1,0:T(8,128)(2,1)S(1)} %collective-permute-done.38.refs_0_, bf16[2,2,256,128]{3,2,1,0:T(8,128)(2,1)S(1)} %collective-permute-done.39.refs_1_, ...), custom_call_target="tpu_custom_call", output_to_operand_aliasing={{0}: (3, {}), {1}: (4, {})} | custom-call | flops 1073741824 | tf_op jit(solution)/shard_map/attn_mid/pallas_call | solution.py:240
  67.0 5.3 %attn_last.1 = (bf16[256,1024]{1,0:T(8,128)(2,1)S(1)}, bf16[4,32,2048]{2,1,0:T(8,128)(2,1)S(1)}, bf16[4,32,2048]{2,1,0:T(8,128)(2,1)S(1)}) custom-call(s32[2]{0:T(128)S(1)} %pad_add_fusion.1.spot, bf16[256,1024]{1,0:T(8,128)(2,1)S(1)} %copy-done, bf16[4,2,256,128]{3,2,1,0:T(8,128)(2,1)S(1)} %collective-permute-done.41.refs_0_, ...), custom_call_target="tpu_custom_call" | custom-call | flops 2147483648 | tf_op jit(solution)/shard_map/attn_last/pallas_call | solution.py:257
  74.9 1.5 %collective-permute-start.43 = (bf16[2,32,2048]{2,1,0:T(8,128)(2,1)S(1)}, bf16[2,32,2048]{2,1,0:T(8,128)(2,1)S(1)}, u32[]{:S(2)}, u32[]{:S(2)}) collective-permute-start(bf16[2,32,2048]{2,1,0:T(8,128)(2,1)S(1)} %get-tuple-element.238), channel_id=1, source_target_pairs={{0,3},{1,0},{2,1},{3,2},{4,7},{5,4},{6,5},{7,6},{8,11},{9,8},{10,9... | collective-permute-start | bytes 786440 | tf_op jit(solution)/shard_map/ppermute | solution.py:293
  76.4 1.5 %collective-permute-start.44 = (bf16[2,32,2048]{2,1,0:T(8,128)(2,1)S(1)}, bf16[2,32,2048]{2,1,0:T(8,128)(2,1)S(1)}, u32[]{:S(2)}, u32[]{:S(2)}) collective-permute-start(bf16[2,32,2048]{2,1,0:T(8,128)(2,1)S(1)} %get-tuple-element.239), channel_id=1, source_target_pairs={{0,2},{1,3},{2,0},{3,1},{4,6},{5,7},{6,4},{7,5},{8,10},{9,11},{10,... | collective-permute-start | bytes 786440 | tf_op jit(solution)/shard_map/ppermute | solution.py:291
  79.2 3.5 %collective-permute-done.42 = bf16[2,32,2048]{2,1,0:T(8,128)(2,1)S(1)} collective-permute-done((bf16[2,32,2048]{2,1,0:T(8,128)(2,1)S(1)}, bf16[2,32,2048]{2,1,0:T(8,128)(2,1)S(1)}, u32[]{:S(2)}, u32[]{:S(2)}) %collective-permute-start.42) | collective-permute-done | bytes 262176 | tf_op jit(solution)/shard_map/ppermute | solution.py:292
  82.8 6.6 %collective-permute-done.44 = bf16[2,32,2048]{2,1,0:T(8,128)(2,1)S(1)} collective-permute-done((bf16[2,32,2048]{2,1,0:T(8,128)(2,1)S(1)}, bf16[2,32,2048]{2,1,0:T(8,128)(2,1)S(1)}, u32[]{:S(2)}, u32[]{:S(2)}) %collective-permute-start.44) | collective-permute-done | bytes 262176 | tf_op jit(solution)/shard_map/ppermute | solution.py:291
  91.7 2.1 %collective-permute-start.48 = (bf16[32,2048]{1,0:T(8,128)(2,1)S(1)}, bf16[32,2048]{1,0:T(8,128)(2,1)S(1)}, u32[]{:S(2)}, u32[]{:S(2)}) collective-permute-start(bf16[32,2048]{1,0:T(8,128)(2,1)S(1)} %get-tuple-element.246), channel_id=1, source_target_pairs={{0,3},{1,0},{2,1},{3,2},{4,7},{5,4},{6,5},{7,6},{8,11},{9,8},{10,9... | collective-permute-start | bytes 393224 | tf_op jit(solution)/shard_map/ppermute | solution.py:297
  93.9 2.3 %collective-permute-done.47 = bf16[32,2048]{1,0:T(8,128)(2,1)S(1)} collective-permute-done((bf16[32,2048]{1,0:T(8,128)(2,1)S(1)}, bf16[32,2048]{1,0:T(8,128)(2,1)S(1)}, u32[]{:S(2)}, u32[]{:S(2)}) %collective-permute-start.47) | collective-permute-done | bytes 131104 | tf_op jit(solution)/shard_map/ppermute | solution.py:296
  97.5 1.9 %collective-permute-done.49 = bf16[32,2048]{1,0:T(8,128)(2,1)S(1)} collective-permute-done((bf16[32,2048]{1,0:T(8,128)(2,1)S(1)}, bf16[32,2048]{1,0:T(8,128)(2,1)S(1)}, u32[]{:S(2)}, u32[]{:S(2)}) %collective-permute-start.49) | collective-permute-done | bytes 131104 | tf_op jit(solution)/shard_map/ppermute | solution.py:298
  (60 shorter events, 18.6 us)
Async XLA Ops:
  1.0 7.2 %collective-permute-start.32 = (bf16[2,4096,128]{2,1,0:T(8,128)(2,1)}, bf16[2,4096,128]{2,1,0:T(8,128)(2,1)S(1)}, u32[]{:S(2)}, u32[]{:S(2)}) collective-permute-start(bf16[2,4096,128]{2,1,0:T(8,128)(2,1)} %bitcast.40), channel_id=1, source_target_pairs={{0,8},{8,0},{16,24},{24,16},{32,40},{40,32},{48,56},{56,48},{64,72... | collective-permute-start | bytes 6291464 | tf_op jit(solution)/shard_map/ppermute | solution.py:321
  9.0 33.3 %copy-start = (bf16[256,1024]{1,0:T(8,128)(2,1)S(1)}, bf16[256,1024]{1,0:T(8,128)(2,1)}, u32[]{:S(2)}) copy-start(bf16[256,1024]{1,0:T(8,128)(2,1)} %q_ref.9) | copy-start | bytes 1572868
  9.0 33.3 %copy-start.2 = (bf16[256,128]{1,0:T(8,128)(2,1)S(1)}, bf16[256,128]{1,0:T(8,128)(2,1)}, u32[]{:S(2)}) copy-start(bf16[256,128]{1,0:T(8,128)(2,1)} %ck.1) | copy-start | bytes 196612
  9.1 7.5 %collective-permute-start.28 = (bf16[2,512,128]{2,1,0:T(8,128)(2,1)S(1)}, bf16[2,512,128]{2,1,0:T(8,128)(2,1)S(1)}, u32[]{:S(2)}, u32[]{:S(2)}) collective-permute-start(bf16[2,512,128]{2,1,0:T(8,128)(2,1)S(1)} %get-tuple-element.154), channel_id=1, source_target_pairs={{16,32},{24,8},{48,64},{56,40},{80,96},{88,72},{112,0},{120,104},{... | collective-permute-start | bytes 786440 | tf_op jit(solution)/shard_map/cond/branch_7_fun/ppermute | solution.py:336
  10.5 6.1 %collective-permute-start.29 = (bf16[2,512,128]{2,1,0:T(8,128)(2,1)S(1)}, bf16[2,512,128]{2,1,0:T(8,128)(2,1)S(1)}, u32[]{:S(2)}, u32[]{:S(2)}) collective-permute-start(bf16[2,512,128]{2,1,0:T(8,128)(2,1)S(1)} %get-tuple-element.155), channel_id=1, source_target_pairs={{48,80},{56,24},{112,16},{120,88},{176,208},{184,152},{240,144},{2... | collective-permute-start | bytes 786440 | tf_op jit(solution)/shard_map/cond/branch_7_fun/ppermute | solution.py:336
  11.2 5.4 %collective-permute-start.30 = (bf16[2,512,128]{2,1,0:T(8,128)(2,1)S(1)}, bf16[2,512,128]{2,1,0:T(8,128)(2,1)S(1)}, u32[]{:S(2)}, u32[]{:S(2)}) collective-permute-start(bf16[2,512,128]{2,1,0:T(8,128)(2,1)S(1)} %get-tuple-element.156), channel_id=1, source_target_pairs={{112,32},{120,72},{240,160},{248,200},{113,33},{121,73},{241,161},... | collective-permute-start | bytes 786440 | tf_op jit(solution)/shard_map/cond/branch_7_fun/ppermute | solution.py:336
  11.9 0.7 collective-permute-start.31
  16.8 3.9 %collective-permute-start.33 = (bf16[2,256,128]{2,1,0:T(8,128)(2,1)S(1)}, bf16[2,256,128]{2,1,0:T(8,128)(2,1)S(1)}, u32[]{:S(2)}, u32[]{:S(2)}) collective-permute-start(bf16[2,256,128]{2,1,0:T(8,128)(2,1)S(1)} %constant_dynamic-slice_fusion), channel_id=1, source_target_pairs={{0,8},{8,0},{16,24},{24,16},{32,40},{40,32},{48,56},{56,48},{64,72... | collective-permute-start | bytes 393224 | tf_op jit(solution)/shard_map/ppermute | solution.py:344
  20.7 6.3 %collective-permute-start.34 = (bf16[2,256,128]{2,1,0:T(8,128)(2,1)S(1)}, bf16[2,256,128]{2,1,0:T(8,128)(2,1)S(1)}, u32[]{:S(2)}, u32[]{:S(2)}) collective-permute-start(bf16[2,256,128]{2,1,0:T(8,128)(2,1)S(1)} %dynamic-slice_select_fusion), channel_id=1, source_target_pairs={{0,128},{8,136},{16,144},{24,152},{32,160},{40,168},{48,176},{56,1... | collective-permute-start | bytes 393224 | tf_op jit(solution)/shard_map/ppermute | solution.py:346
  27.0 17.8 %collective-permute-start.35 = (bf16[1,2,256,128]{3,2,1,0:T(8,128)(2,1)S(1)}, bf16[1,2,256,128]{3,2,1,0:T(8,128)(2,1)S(1)}, u32[]{:S(2)}, u32[]{:S(2)}) collective-permute-start(bf16[1,2,256,128]{3,2,1,0:T(8,128)(2,1)S(1)} %select_bitcast_fusion.a0), channel_id=1, source_target_pairs={{0,112},{8,120},{16,0},{24,8},{32,16},{40,24},{48,32},{56,40},{64,... | collective-permute-start | bytes 393224 | tf_op jit(solution)/shard_map/ppermute | solution.py:350
  36.2 8.6 %collective-permute-start.36 = (bf16[1,2,256,128]{3,2,1,0:T(8,128)(2,1)S(1)}, bf16[1,2,256,128]{3,2,1,0:T(8,128)(2,1)S(1)}, u32[]{:S(2)}, u32[]{:S(2)}) collective-permute-start(bf16[1,2,256,128]{3,2,1,0:T(8,128)(2,1)S(1)} %select_bitcast_fusion.a0), channel_id=1, source_target_pairs={{0,16},{8,24},{16,32},{24,40},{32,48},{40,56},{48,64},{56,72},{64,... | collective-permute-start | bytes 393224 | tf_op jit(solution)/shard_map/ppermute | solution.py:351
  36.2 12.4 %collective-permute-start.37 = (bf16[1,2,256,128]{3,2,1,0:T(8,128)(2,1)S(1)}, bf16[1,2,256,128]{3,2,1,0:T(8,128)(2,1)S(1)}, u32[]{:S(2)}, u32[]{:S(2)}) collective-permute-start(bf16[1,2,256,128]{3,2,1,0:T(8,128)(2,1)S(1)} %select_bitcast_fusion.a0), channel_id=1, source_target_pairs={{0,64},{8,72},{16,80},{24,88},{32,96},{40,104},{48,112},{56,120},{... | collective-permute-start | bytes 393224 | tf_op jit(solution)/shard_map/ppermute | solution.py:349
  48.7 8.5 %collective-permute-start.40 = (bf16[4,2,256,128]{3,2,1,0:T(8,128)(2,1)S(1)}, bf16[4,2,256,128]{3,2,1,0:T(8,128)(2,1)S(1)}, u32[]{:S(2)}, u32[]{:S(2)}) collective-permute-start(bf16[4,2,256,128]{3,2,1,0:T(8,128)(2,1)S(1)} %pad_maximum_fusion), channel_id=1, source_target_pairs={{0,8},{8,0},{16,24},{24,16},{32,40},{40,32},{48,56},{56,48},{64,72... | collective-permute-start | bytes 1572872 | tf_op jit(solution)/shard_map/ppermute | solution.py:357
  52.6 8.5 %collective-permute-start.38 = (bf16[2,2,256,128]{3,2,1,0:T(8,128)(2,1)S(1)}, bf16[2,2,256,128]{3,2,1,0:T(8,128)(2,1)S(1)}, u32[]{:S(2)}, u32[]{:S(2)}) collective-permute-start(bf16[2,2,256,128]{3,2,1,0:T(8,128)(2,1)S(1)} %get-tuple-element.248), channel_id=1, source_target_pairs={{0,112},{8,120},{16,0},{24,8},{32,16},{40,24},{48,32},{56,40},{64,... | collective-permute-start | bytes 786440 | tf_op jit(solution)/shard_map/ppermute | solution.py:355
  52.7 9.3 %collective-permute-start.39 = (bf16[2,2,256,128]{3,2,1,0:T(8,128)(2,1)S(1)}, bf16[2,2,256,128]{3,2,1,0:T(8,128)(2,1)S(1)}, u32[]{:S(2)}, u32[]{:S(2)}) collective-permute-start(bf16[2,2,256,128]{3,2,1,0:T(8,128)(2,1)S(1)} %get-tuple-element.247), channel_id=1, source_target_pairs={{0,16},{8,24},{16,32},{24,40},{32,48},{40,56},{48,64},{56,72},{64,... | collective-permute-start | bytes 786440 | tf_op jit(solution)/shard_map/ppermute | solution.py:356
  62.0 5.0 %collective-permute-start.41 = (bf16[4,2,256,128]{3,2,1,0:T(8,128)(2,1)S(1)}, bf16[4,2,256,128]{3,2,1,0:T(8,128)(2,1)S(1)}, u32[]{:S(2)}, u32[]{:S(2)}) collective-permute-start(bf16[4,2,256,128]{3,2,1,0:T(8,128)(2,1)S(1)} %pad_maximum_fusion.1), channel_id=1, source_target_pairs={{0,8},{8,0},{16,24},{24,16},{32,40},{40,32},{48,56},{56,48},{64,72... | collective-permute-start | bytes 1572872 | tf_op jit(solution)/shard_map/ppermute | solution.py:362
  73.6 9.1 %collective-permute-start.42 = (bf16[2,32,2048]{2,1,0:T(8,128)(2,1)S(1)}, bf16[2,32,2048]{2,1,0:T(8,128)(2,1)S(1)}, u32[]{:S(2)}, u32[]{:S(2)}) collective-permute-start(bf16[2,32,2048]{2,1,0:T(8,128)(2,1)S(1)} %get-tuple-element.237), channel_id=1, source_target_pairs={{0,1},{1,2},{2,3},{3,0},{4,5},{5,6},{6,7},{7,4},{8,9},{9,10},{10,1... | collective-permute-start | bytes 786440 | tf_op jit(solution)/shard_map/ppermute | solution.py:292
  74.9 7.8 %collective-permute-start.43 = (bf16[2,32,2048]{2,1,0:T(8,128)(2,1)S(1)}, bf16[2,32,2048]{2,1,0:T(8,128)(2,1)S(1)}, u32[]{:S(2)}, u32[]{:S(2)}) collective-permute-start(bf16[2,32,2048]{2,1,0:T(8,128)(2,1)S(1)} %get-tuple-element.238), channel_id=1, source_target_pairs={{0,3},{1,0},{2,1},{3,2},{4,7},{5,4},{6,5},{7,6},{8,11},{9,8},{10,9... | collective-permute-start | bytes 786440 | tf_op jit(solution)/shard_map/ppermute | solution.py:293
  76.4 13.0 %collective-permute-start.44 = (bf16[2,32,2048]{2,1,0:T(8,128)(2,1)S(1)}, bf16[2,32,2048]{2,1,0:T(8,128)(2,1)S(1)}, u32[]{:S(2)}, u32[]{:S(2)}) collective-permute-start(bf16[2,32,2048]{2,1,0:T(8,128)(2,1)S(1)} %get-tuple-element.239), channel_id=1, source_target_pairs={{0,2},{1,3},{2,0},{3,1},{4,6},{5,7},{6,4},{7,5},{8,10},{9,11},{10,... | collective-permute-start | bytes 786440 | tf_op jit(solution)/shard_map/ppermute | solution.py:291
  77.9 13.0 %collective-permute-start.46 = (bf16[4,32,2048]{2,1,0:T(8,128)(2,1)S(1)}, bf16[4,32,2048]{2,1,0:T(8,128)(2,1)S(1)}, u32[]{:S(2)}, u32[]{:S(2)}) collective-permute-start(bf16[4,32,2048]{2,1,0:T(8,128)(2,1)S(1)} %get-tuple-element.241), channel_id=1, source_target_pairs={{0,4},{1,5},{2,6},{3,7},{4,0},{5,1},{6,2},{7,3},{8,12},{9,13},{10,... | collective-permute-start | bytes 1572872 | tf_op jit(solution)/shard_map/ppermute | solution.py:289
  89.5 4.3 %collective-permute-start.45 = (bf16[32,2048]{1,0:T(8,128)(2,1)S(1)}, bf16[32,2048]{1,0:T(8,128)(2,1)S(1)}, u32[]{:S(2)}, u32[]{:S(2)}) collective-permute-start(bf16[32,2048]{1,0:T(8,128)(2,1)S(1)} %fusion.22), channel_id=1, source_target_pairs={{0,4},{1,5},{2,6},{3,7},{4,0},{5,1},{6,2},{7,3},{8,12},{9,13},{10,... | collective-permute-start | bytes 393224 | tf_op jit(solution)/shard_map/ppermute | solution.py:300
  91.1 5.1 %collective-permute-start.47 = (bf16[32,2048]{1,0:T(8,128)(2,1)S(1)}, bf16[32,2048]{1,0:T(8,128)(2,1)S(1)}, u32[]{:S(2)}, u32[]{:S(2)}) collective-permute-start(bf16[32,2048]{1,0:T(8,128)(2,1)S(1)} %get-tuple-element.244), channel_id=1, source_target_pairs={{0,1},{1,2},{2,3},{3,0},{4,5},{5,6},{6,7},{7,4},{8,9},{9,10},{10,1... | collective-permute-start | bytes 393224 | tf_op jit(solution)/shard_map/ppermute | solution.py:296
  91.7 5.8 %collective-permute-start.48 = (bf16[32,2048]{1,0:T(8,128)(2,1)S(1)}, bf16[32,2048]{1,0:T(8,128)(2,1)S(1)}, u32[]{:S(2)}, u32[]{:S(2)}) collective-permute-start(bf16[32,2048]{1,0:T(8,128)(2,1)S(1)} %get-tuple-element.246), channel_id=1, source_target_pairs={{0,3},{1,0},{2,1},{3,2},{4,7},{5,4},{6,5},{7,6},{8,11},{9,8},{10,9... | collective-permute-start | bytes 393224 | tf_op jit(solution)/shard_map/ppermute | solution.py:297
  93.8 5.6 %collective-permute-start.49 = (bf16[32,2048]{1,0:T(8,128)(2,1)S(1)}, bf16[32,2048]{1,0:T(8,128)(2,1)S(1)}, u32[]{:S(2)}, u32[]{:S(2)}) collective-permute-start(bf16[32,2048]{1,0:T(8,128)(2,1)S(1)} %get-tuple-element.245), channel_id=1, source_target_pairs={{0,2},{1,3},{2,0},{3,1},{4,6},{5,7},{6,4},{7,5},{8,10},{9,11},{10,... | collective-permute-start | bytes 393224 | tf_op jit(solution)/shard_map/ppermute | solution.py:298
  (5 other events, 96.4 us)

commit v2 on v1

--- a/solution.py
+++ b/solution.py
@@ -87,11 +87,12 @@
     return pl.ds(pl.multiple_of(h * HD, HD), HD)
 
 
-def first_kernel(lens, q_ref, ck, cv, a0, m_out, acc_out):
+def first_kernel(lens, q_ref, ck, cv, *refs):
+    m_out, acc_out = refs[-2:]
     rows = q_ref.shape[0]
 
     def head(h):
-        keys, values = pieces([a0])
+        keys, values = pieces(refs[:-2])
         slot = lax.broadcasted_iota(jnp.int32, (rows, 128), 0) // CLEN
         lane = lax.broadcasted_iota(jnp.int32, (rows, 128), 1)
         mask = [(slot == t) & (lane < lens[t]) for t in range(2)]
@@ -100,7 +101,7 @@
             q, [ck[...]] + keys, [cv[...]] + values, [mask] + [None] * len(keys), None, None
         )
 
-    each_head(head, 4)
+    each_head(head, 2)
 
 
 def mid_kernel(n, q_ref, *refs):
@@ -130,28 +131,37 @@
         _, acc = absorb(q, keys, values, [None] * len(keys), m_in[h], acc_in[h])
         ctx[:, head_cols(h)] = (acc[:, :HD] / acc[:, HD:]).astype(jnp.bfloat16)
 
-    each_head(head, 4)
+    each_head(head)
 
     tile = own_b.shape[1]
     half = own_b.shape[2]
     tp_of = [((spot[0] + dy) % 2) * 4 + (spot[1] + dx) % 4 for dy in range(2) for dx in range(4)]
     rel = jnp.concatenate([ctx[pl.ds(pl.multiple_of(t * tile, tile), tile)] for t in tp_of], axis=0)
     rel_out[...] = rel
-    for c in range(0, half, W_BLOCK):
-        y = product(rel, w, half + c)
+
+    def block(i, carry):
+        c = pl.multiple_of(i * W_BLOCK, W_BLOCK)
+        y = product(rel_out[...], w, half + c)
         for dy, ref in enumerate((own_b, yb)):
             for dx in range(4):
                 ref[dx, :, pl.ds(c, W_BLOCK)] = y[(dy * 4 + dx) * tile : (dy * 4 + dx + 1) * tile]
+        return carry
+
+    lax.fori_loop(0, half // W_BLOCK, block, 0, unroll=2)
 
 
 def left_kernel(rel_ref, w, own_a, x1, x2, x3):
     tile = own_a.shape[1]
-    rel = rel_ref[...]
-    for c in range(0, own_a.shape[2], W_BLOCK):
-        y = product(rel, w, c)
+
+    def block(i, carry):
+        c = pl.multiple_of(i * W_BLOCK, W_BLOCK)
+        y = product(rel_ref[...], w, c)
         for dx, ref in enumerate((own_a, x1, x2, x3)):
             for dy in range(2):
                 ref[dy, :, pl.ds(c, W_BLOCK)] = y[(dy * 4 + dx) * tile : (dy * 4 + dx + 1) * tile]
+        return carry
+
+    lax.fori_loop(0, own_a.shape[2] // W_BLOCK, block, 0, unroll=2)
 
 
 VM = pl.BlockSpec(memory_space=pltpu.VMEM)
@@ -176,62 +186,65 @@
     return sum(a.shape[0] for a in kvs) * PIECE
 
 
-def moves(pairs, sem):
-    copies = [pltpu.make_async_copy(source, target, sem.at[i]) for i, (source, target) in enumerate(pairs)]
+def windows(at):
+    z, c = at[1], at[2]
+    up = 1 - 2 * c
+    spots = [(z * 2 * PIECE + c * PIECE, PIECE)]
+    spots += [(lax.rem(z + up * d + 8, 8) * 2 * PIECE, 2 * PIECE) for d in (1, 2, 3)]
+    spots.append((lax.rem(z + 4, 8) * 2 * PIECE + c * PIECE, PIECE))
+    return [pl.ds(pl.multiple_of(start, PIECE), size) for start, size in spots]
+
+
+def cut_kernel(at, prefix, *refs):
+    outs, sem = refs[:5], refs[5]
+    copies = [
+        pltpu.make_async_copy(prefix.at[:, rows], ref, sem.at[i])
+        for i, (rows, ref) in enumerate(zip(windows(at), outs))
+    ]
     for copy in copies:
         copy.start()
     for copy in copies:
         copy.wait()
 
 
-def windows(at, source):
-    z, c = at[1], at[2]
-    up = 1 - 2 * c
-    spots = [(lax.rem(z + up * d + 8, 8) * 2 * PIECE, 2 * PIECE) for d in range(4)]
-    spots.append((lax.rem(z + 4, 8) * 2 * PIECE + c * PIECE, PIECE))
-    return [source.at[:, pl.ds(pl.multiple_of(start, PIECE), size)] for start, size in spots]
-
-
-def cut_kernel(at, prefix, *refs):
-    moves(zip(windows(at, prefix), refs[:-1]), refs[-1])
-
-
 def choose_kernel(at, partner, *refs):
-    mine, outs, sem = refs[:5], refs[5:10], refs[10]
+    mine, outs = refs[:5], refs[5:]
 
     @pl.when(at[0] == 1)
     def _():
-        moves(zip(mine, outs), sem)
+        for ref, out in zip(mine, outs):
+            out[...] = ref[...]
 
     @pl.when(at[0] == 0)
     def _():
-        moves(zip(windows(at, partner), outs), sem)
+        for rows, out in zip(windows(at), outs):
+            out[...] = partner[:, rows, :]
 
 
 def cut_call(kernel, at, source, *mine):
     part = lambda size: jax.ShapeDtypeStruct((2, size, HD), jnp.bfloat16)
     return pl.pallas_call(
         kernel,
-        out_shape=(part(2 * PIECE),) * 4 + (part(PIECE),),
-        in_specs=[SM] + [ANY] * (1 + len(mine)),
+        out_shape=(part(PIECE),) + (part(2 * PIECE),) * 3 + (part(PIECE),),
+        in_specs=[SM] + [VM if mine else ANY] * (1 + len(mine)),
         out_specs=(VM,) * 5,
-        scratch_shapes=[pltpu.SemaphoreType.DMA((5,))],
+        scratch_shapes=[] if mine else [pltpu.SemaphoreType.DMA((5,))],
         compiler_params=pltpu.CompilerParams(vmem_limit_bytes=4 << 20),
         cost_estimate=pl.CostEstimate(flops=1 << 28, transcendentals=0, bytes_accessed=0),
     )(at, source, *mine)
 
 
-def first_call(lens, q, ck, cv, a0):
+def first_call(lens, q, ck, cv, kvs):
     rows = q.shape[0]
     return pl.pallas_call(
         first_kernel,
         out_shape=state_shapes(rows),
-        in_specs=[SM] + [VM] * 4,
+        in_specs=[SM] + [VM] * (3 + len(kvs)),
         out_specs=(VM, VM),
-        cost_estimate=cost(rows, 2 * PIECE),
+        cost_estimate=cost(rows, PIECE + key_count(kvs)),
         compiler_params=pltpu.CompilerParams(vmem_limit_bytes=12 << 20),
         name="attn_first",
-    )(lens, q, ck, cv, a0)
+    )(lens, q, ck, cv, *kvs)
 
 
 def mid_call(q, kvs, state):
@@ -315,8 +328,9 @@
     cut_at = jnp.stack([my_c == root_c, my_z, my_c]).astype(jnp.int32)
     steps = (my_z - root_z) % 8
     steps = jnp.where(my_c == 0, steps, (8 - steps) % 8)
-    prefix, cut_at, spot, steps, root_z, root_yh, my_c, my_yh = lax.optimization_barrier(
-        (prefix_kv[0], cut_at, spot, steps, root_z, root_yh, my_c, my_yh)
+    prefix = prefix_kv[0]
+    cut_at, spot, steps, root_z, root_yh, my_c, my_yh = lax.optimization_barrier(
+        (cut_at, spot, steps, root_z, root_yh, my_c, my_yh)
     )
     partner = over_rep(prefix, perm=CORE_SWAP)
     parts = cut_call(cut_kernel, cut_at, prefix)
@@ -334,8 +348,9 @@
                     for c in range(2)
                 ]
                 got[d] = over_rep(parts[d - 1], perm=pairs)
-            got[4] = jnp.concatenate([got[4], got[4]], axis=1)
-            return lax.select_n(jnp.minimum(steps, 4), own, got[1], got[2], got[3], got[4])
+            twice = lambda a: jnp.concatenate([a, a], axis=1)
+            got[4] = twice(got[4])
+            return lax.select_n(jnp.minimum(steps, 4), twice(own), got[1], got[2], got[3], got[4])
 
         return send
 
@@ -349,12 +364,13 @@
     facing = over_rep(a0, perm=z_shift(4))
     above = over_rep(a0, perm=z_shift(-1))
     below = over_rep(a0, perm=z_shift(1))
-    state = first_call(lengths[0], queries, cand_keys, cand_values, a0)
+    own_other = over_rep(a0, perm=CORE_SWAP)
+    state = first_call(lengths[0], queries, cand_keys, cand_values, [a0, own_other])
     above, below, facing, state = lax.optimization_barrier((above, below, facing, state))
 
     far_above = over_rep(jnp.concatenate([above, facing]), perm=z_shift(-1))
     far_below = over_rep(jnp.concatenate([below, facing]), perm=z_shift(1))
-    near_other = over_rep(jnp.concatenate([a0, above, below, facing]), perm=CORE_SWAP)
+    near_other = over_rep(jnp.concatenate([above, below, facing]), perm=CORE_SWAP)
     state = mid_call(queries, [above, below, facing], state)
     state = mid_call(queries, [near_other], state)
     far_above, far_below, state = lax.optimization_barrier((far_above, far_below, state))

time: 102 us -> 101 us (level)
  starting transfers between devices: 44.1 us -> 42.2 us
    pallas_call x1, Pallas kernels: 2.49 us -> 4.35 us  [first_call(): pl.pallas_call(first_kernel, out_shape=state_shapes(rows), in_specs=[SM]...]
    ppermute x1 -> x2, starting transfers between devices: 3.86 us -> 2.35 us  [the longest x1 1.3 us: body(): own_other = over_rep(a0, perm=CORE_SWAP)]
  transfers between devices with their start and end apart: 22 -> 23, of which waited for: 11 -> 12; matrix products, arithmetic and copies ran while one was open for 0% -> 1% of each run, Pallas kernels for 14% -> 15%
where the time goes in v2:
time: 101 us; the launch traced here: 99.9 us
  starting transfers between devices  42.2 us (42%)
  waiting for transfers between devices  31.1 us (31%)
  Pallas kernels  22 us (22%)
  local copies, waits for them, and re-layouts  1.7 us (2%)
  other arithmetic  1.6 us (2%)
  between operations  1.08 us (1%)
    pallas_call x3, Pallas kernels, mid_call(): pl.pallas_call(functools.partial(mid_kernel, n), out_shape=state_shapes(r...  9.78 us
    ppermute x1, starting transfers between devices, body(): above = over_rep(a0, perm=z_shift(-1))  9.1 us
    ppermute x1, waiting for transfers between devices, reduce_rows(): r2 = over_tp(x2, perm=x_shift(2))  6.6 us
    ppermute x1, starting transfers between devices, body(): facing = over_rep(a0, perm=z_shift(4))  6.07 us
    pallas_call x1, Pallas kernels, last_call(): pl.pallas_call(functools.partial(last_kernel, n), out_shape=outs, in_spec...  5.01 us
    ppermute x1, waiting for transfers between devices, body(): facing = over_rep(a0, perm=z_shift(4))  4.68 us
    pallas_call x1, Pallas kernels, first_call(): pl.pallas_call(first_kernel, out_shape=state_shapes(rows), in_specs=[SM]...  4.35 us
    ppermute x4, waiting for transfers between devices, send(): got[d] = over_rep(parts[d - 1], perm=pairs)  4.05 us
  transfers between devices with their start and end apart: 23, of which 12 were waited for; matrix products, arithmetic and copies ran while one was open for 1% of the time, Pallas kernels for 15%

profile of v2, /device:TPU:1, one launch (start us, length us, event | category | flops | bytes accessed | tf_op | source)
XLA Modules:
  0.0 99.9 jit_solution(17767057270455385291)
XLA Ops:
  0.0 3.2 %collective-permute-start.32 = (bf16[2,4096,128]{2,1,0:T(8,128)(2,1)}, bf16[2,4096,128]{2,1,0:T(8,128)(2,1)S(1)}, u32[]{:S(2)}, u32[]{:S(2)}) collective-permute-start(bf16[2,4096,128]{2,1,0:T(8,128)(2,1)} %bitcast.40), channel_id=1, source_target_pairs={{0,8},{8,0},{16,24},{24,16},{32,40},{40,32},{48,56},{56,48},{64,72... | collective-permute-start | bytes 6291464 | tf_op jit(solution)/shard_map/ppermute | solution.py:335
  4.2 1.6 %copy-done.1 = bf16[1,2,4096,128]{3,2,1,0:T(8,128)(2,1)S(1)} copy-done((bf16[1,2,4096,128]{3,2,1,0:T(8,128)(2,1)S(1)}, bf16[1,2,4096,128]{3,2,1,0:T(8,128)(2,1)}, u32[]{:S(2)}) %copy-start.1) | copy-done | bytes 2097176
  7.9 7.8 %conditional.1 = (bf16[2,512,128]{2,1,0:T(8,128)(2,1)S(1)}) conditional(s32[]{:T(128)} %clamp.3, (s32[]{:T(128)}, bf16[2,256,128]{2,1,0:T(8,128)(2,1)S(1)}, bf16[2,512,128]{2,1,0:T(8,128)(2,1)S(1)}, bf16[2,512,128]{2,1,0:T(8,128)(2,1)S(1)}, bf16[2,512,128]{2,1,0:T(8,128)(2,1)S(1)}, ...), branch_computations={%region_0.1_spmd, %region_1.2_spmd, %region_2.3_spmd, %region_3.4_... | conditional | flops 1572869 | bytes 4980956 | solution.py:357
  11.4 4.0 %collective-permute-done.28 = bf16[2,512,128]{2,1,0:T(8,128)(2,1)S(1)} collective-permute-done((bf16[2,512,128]{2,1,0:T(8,128)(2,1)S(1)}, bf16[2,512,128]{2,1,0:T(8,128)(2,1)S(1)}, u32[]{:S(2)}, u32[]{:S(2)}) %collective-permute-start.28) | collective-permute-done | bytes 262176 | tf_op jit(solution)/shard_map/cond/branch_7_fun/ppermute | solution.py:350
  15.7 2.8 %collective-permute-start.33 = (bf16[2,256,128]{2,1,0:T(8,128)(2,1)S(1)}, bf16[2,256,128]{2,1,0:T(8,128)(2,1)S(1)}, u32[]{:S(2)}, u32[]{:S(2)}) collective-permute-start(bf16[2,256,128]{2,1,0:T(8,128)(2,1)S(1)} %constant_dynamic-slice_fusion), channel_id=1, source_target_pairs={{0,8},{8,0},{16,24},{24,16},{32,40},{40,32},{48,56},{56,48},{64,72... | collective-permute-start | bytes 393224 | tf_op jit(solution)/shard_map/ppermute | solution.py:359
  19.5 3.0 %collective-permute-start.34 = (bf16[2,256,128]{2,1,0:T(8,128)(2,1)S(1)}, bf16[2,256,128]{2,1,0:T(8,128)(2,1)S(1)}, u32[]{:S(2)}, u32[]{:S(2)}) collective-permute-start(bf16[2,256,128]{2,1,0:T(8,128)(2,1)S(1)} %dynamic-slice_select_fusion), channel_id=1, source_target_pairs={{0,128},{8,136},{16,144},{24,152},{32,160},{40,168},{48,176},{56,1... | collective-permute-start | bytes 393224 | tf_op jit(solution)/shard_map/ppermute | solution.py:361
  22.5 3.3 %collective-permute-done.34 = bf16[2,256,128]{2,1,0:T(8,128)(2,1)S(1)} collective-permute-done((bf16[2,256,128]{2,1,0:T(8,128)(2,1)S(1)}, bf16[2,256,128]{2,1,0:T(8,128)(2,1)S(1)}, u32[]{:S(2)}, u32[]{:S(2)}) %collective-permute-start.34) | collective-permute-done | bytes 131104 | tf_op jit(solution)/shard_map/ppermute | solution.py:361
  27.1 9.1 %collective-permute-start.35 = (bf16[1,2,256,128]{3,2,1,0:T(8,128)(2,1)S(1)}, bf16[1,2,256,128]{3,2,1,0:T(8,128)(2,1)S(1)}, u32[]{:S(2)}, u32[]{:S(2)}) collective-permute-start(bf16[1,2,256,128]{3,2,1,0:T(8,128)(2,1)S(1)} %select_bitcast_fusion.refs_0_), channel_id=1, source_target_pairs={{0,112},{8,120},{16,0},{24,8},{32,16},{40,24},{48,32},{56,40},{64,... | collective-permute-start | bytes 393224 | tf_op jit(solution)/shard_map/ppermute | solution.py:365
  36.2 6.1 %collective-permute-start.37 = (bf16[1,2,256,128]{3,2,1,0:T(8,128)(2,1)S(1)}, bf16[1,2,256,128]{3,2,1,0:T(8,128)(2,1)S(1)}, u32[]{:S(2)}, u32[]{:S(2)}) collective-permute-start(bf16[1,2,256,128]{3,2,1,0:T(8,128)(2,1)S(1)} %select_bitcast_fusion.refs_0_), channel_id=1, source_target_pairs={{0,64},{8,72},{16,80},{24,88},{32,96},{40,104},{48,112},{56,120},{... | collective-permute-start | bytes 393224 | tf_op jit(solution)/shard_map/ppermute | solution.py:364
  42.4 4.3 %attn_first.1 = (f32[8,256,128]{2,1,0:T(8,128)S(1)}, f32[8,256,256]{2,1,0:T(8,128)S(1)}) custom-call(s32[2]{0:T(128)S(1)} %bitcast.42, bf16[256,1024]{1,0:T(8,128)(2,1)S(1)} %copy-done, bf16[256,128]{1,0:T(8,128)(2,1)S(1)} %copy-done.2, bf16[256,128]{1,0:T(8,128)(2,1)S(1)} %copy-done.3, bf16[1,2,256,128]{3,2,1,0:T(8,128)(2,1)S(1)} %select_bitcast_fusion.refs_0_, ...), custom_call_target="tpu_custom_call" | custom-call | flops 805306368 | tf_op jit(solution)/shard_map/attn_first/pallas_call | solution.py:239
  46.7 4.7 %collective-permute-done.37.refs_2_ = bf16[1,2,256,128]{3,2,1,0:T(8,128)(2,1)S(1)} collective-permute-done((bf16[1,2,256,128]{3,2,1,0:T(8,128)(2,1)S(1)}, bf16[1,2,256,128]{3,2,1,0:T(8,128)(2,1)S(1)}, u32[]{:S(2)}, u32[]{:S(2)}) %collective-permute-start.37) | collective-permute-done | bytes 131104 | tf_op jit(solution)/shard_map/ppermute | solution.py:364
  52.7 1.5 %collective-permute-start.40 = (bf16[2,2,256,128]{3,2,1,0:T(8,128)(2,1)S(1)}, bf16[2,2,256,128]{3,2,1,0:T(8,128)(2,1)S(1)}, u32[]{:S(2)}, u32[]{:S(2)}) collective-permute-start(bf16[2,2,256,128]{3,2,1,0:T(8,128)(2,1)S(1)} %get-tuple-element.245), channel_id=1, source_target_pairs={{0,16},{8,24},{16,32},{24,40},{32,48},{40,56},{48,64},{56,72},{64,... | collective-permute-start | bytes 786440 | tf_op jit(solution)/shard_map/ppermute | solution.py:372
  54.1 3.1 %attn_mid.3 = (f32[8,256,128]{2,1,0:T(8,128)S(1)}, f32[8,256,256]{2,1,0:T(8,128)S(1)}) custom-call(bf16[256,1024]{1,0:T(8,128)(2,1)S(1)} %copy-done, bf16[1,2,256,128]{3,2,1,0:T(8,128)(2,1)S(1)} %collective-permute-done.35.refs_0_, bf16[1,2,256,128]{3,2,1,0:T(8,128)(2,1)S(1)} %collective-permute-done.36.refs_1_, ...), custom_call_target="tpu_custom_call", output_to_operand_aliasing={{0}: (4, {}), {1}: (5, {})} | custom-call | flops 805306368 | tf_op jit(solution)/shard_map/attn_mid/pallas_call | solution.py:253
  57.2 3.0 %attn_mid.4 = (f32[8,256,128]{2,1,0:T(8,128)S(1)}, f32[8,256,256]{2,1,0:T(8,128)S(1)}) custom-call(bf16[256,1024]{1,0:T(8,128)(2,1)S(1)} %copy-done, bf16[3,2,256,128]{3,2,1,0:T(8,128)(2,1)S(1)} %collective-permute-done.41.refs_0_, f32[8,256,128]{2,1,0:T(8,128)S(1)} %get-tuple-element.223.refs_1_, ...), custom_call_target="tpu_custom_call", output_to_operand_aliasing={{0}: (2, {}), {1}: (3, {})} | custom-call | flops 805306368 | tf_op jit(solution)/shard_map/attn_mid/pallas_call | solution.py:253
  60.5 1.5 %collective-permute-done.40.refs_1_ = bf16[2,2,256,128]{3,2,1,0:T(8,128)(2,1)S(1)} collective-permute-done((bf16[2,2,256,128]{3,2,1,0:T(8,128)(2,1)S(1)}, bf16[2,2,256,128]{3,2,1,0:T(8,128)(2,1)S(1)}, u32[]{:S(2)}, u32[]{:S(2)}) %collective-permute-start.40) | collective-permute-done | bytes 262176 | tf_op jit(solution)/shard_map/ppermute | solution.py:372
  63.0 3.8 %attn_mid.5 = (f32[8,256,128]{2,1,0:T(8,128)S(1)}, f32[8,256,256]{2,1,0:T(8,128)S(1)}) custom-call(bf16[256,1024]{1,0:T(8,128)(2,1)S(1)} %copy-done, bf16[2,2,256,128]{3,2,1,0:T(8,128)(2,1)S(1)} %collective-permute-done.39.refs_0_, bf16[2,2,256,128]{3,2,1,0:T(8,128)(2,1)S(1)} %collective-permute-done.40.refs_1_, ...), custom_call_target="tpu_custom_call", output_to_operand_aliasing={{0}: (3, {}), {1}: (4, {})} | custom-call | flops 1073741824 | tf_op jit(solution)/shard_map/attn_mid/pallas_call | solution.py:253
  66.8 5.0 %attn_last.1 = (bf16[256,1024]{1,0:T(8,128)(2,1)S(1)}, bf16[4,32,2048]{2,1,0:T(8,128)(2,1)S(1)}, bf16[4,32,2048]{2,1,0:T(8,128)(2,1)S(1)}) custom-call(s32[2]{0:T(128)S(1)} %pad_add_fusion.1.spot, bf16[256,1024]{1,0:T(8,128)(2,1)S(1)} %copy-done, bf16[4,2,256,128]{3,2,1,0:T(8,128)(2,1)S(1)} %collective-permute-done.42.refs_0_, ...), custom_call_target="tpu_custom_call" | custom-call | flops 2147483648 | tf_op jit(solution)/shard_map/attn_last/pallas_call | solution.py:270
  74.6 1.5 %collective-permute-start.44 = (bf16[2,32,2048]{2,1,0:T(8,128)(2,1)S(1)}, bf16[2,32,2048]{2,1,0:T(8,128)(2,1)S(1)}, u32[]{:S(2)}, u32[]{:S(2)}) collective-permute-start(bf16[2,32,2048]{2,1,0:T(8,128)(2,1)S(1)} %get-tuple-element.236), channel_id=1, source_target_pairs={{0,3},{1,0},{2,1},{3,2},{4,7},{5,4},{6,5},{7,6},{8,11},{9,8},{10,9... | collective-permute-start | bytes 786440 | tf_op jit(solution)/shard_map/ppermute | solution.py:306
  76.0 1.5 %collective-permute-start.45 = (bf16[2,32,2048]{2,1,0:T(8,128)(2,1)S(1)}, bf16[2,32,2048]{2,1,0:T(8,128)(2,1)S(1)}, u32[]{:S(2)}, u32[]{:S(2)}) collective-permute-start(bf16[2,32,2048]{2,1,0:T(8,128)(2,1)S(1)} %get-tuple-element.237), channel_id=1, source_target_pairs={{0,2},{1,3},{2,0},{3,1},{4,6},{5,7},{6,4},{7,5},{8,10},{9,11},{10,... | collective-permute-start | bytes 786440 | tf_op jit(solution)/shard_map/ppermute | solution.py:304
  78.8 3.6 %collective-permute-done.43 = bf16[2,32,2048]{2,1,0:T(8,128)(2,1)S(1)} collective-permute-done((bf16[2,32,2048]{2,1,0:T(8,128)(2,1)S(1)}, bf16[2,32,2048]{2,1,0:T(8,128)(2,1)S(1)}, u32[]{:S(2)}, u32[]{:S(2)}) %collective-permute-start.43) | collective-permute-done | bytes 262176 | tf_op jit(solution)/shard_map/ppermute | solution.py:305
  82.4 6.6 %collective-permute-done.45 = bf16[2,32,2048]{2,1,0:T(8,128)(2,1)S(1)} collective-permute-done((bf16[2,32,2048]{2,1,0:T(8,128)(2,1)S(1)}, bf16[2,32,2048]{2,1,0:T(8,128)(2,1)S(1)}, u32[]{:S(2)}, u32[]{:S(2)}) %collective-permute-start.45) | collective-permute-done | bytes 262176 | tf_op jit(solution)/shard_map/ppermute | solution.py:304
  91.4 2.1 %collective-permute-start.49 = (bf16[32,2048]{1,0:T(8,128)(2,1)S(1)}, bf16[32,2048]{1,0:T(8,128)(2,1)S(1)}, u32[]{:S(2)}, u32[]{:S(2)}) collective-permute-start(bf16[32,2048]{1,0:T(8,128)(2,1)S(1)} %get-tuple-element.244), channel_id=1, source_target_pairs={{0,3},{1,0},{2,1},{3,2},{4,7},{5,4},{6,5},{7,6},{8,11},{9,8},{10,9... | collective-permute-start | bytes 393224 | tf_op jit(solution)/shard_map/ppermute | solution.py:310
  93.5 2.3 %collective-permute-done.48 = bf16[32,2048]{1,0:T(8,128)(2,1)S(1)} collective-permute-done((bf16[32,2048]{1,0:T(8,128)(2,1)S(1)}, bf16[32,2048]{1,0:T(8,128)(2,1)S(1)}, u32[]{:S(2)}, u32[]{:S(2)}) %collective-permute-start.48) | collective-permute-done | bytes 131104 | tf_op jit(solution)/shard_map/ppermute | solution.py:309
  97.2 1.9 %collective-permute-done.50 = bf16[32,2048]{1,0:T(8,128)(2,1)S(1)} collective-permute-done((bf16[32,2048]{1,0:T(8,128)(2,1)S(1)}, bf16[32,2048]{1,0:T(8,128)(2,1)S(1)}, u32[]{:S(2)}, u32[]{:S(2)}) %collective-permute-start.50) | collective-permute-done | bytes 131104 | tf_op jit(solution)/shard_map/ppermute | solution.py:311
  (62 shorter events, 19.4 us)
Async XLA Ops:
  0.0 7.2 %collective-permute-start.32 = (bf16[2,4096,128]{2,1,0:T(8,128)(2,1)}, bf16[2,4096,128]{2,1,0:T(8,128)(2,1)S(1)}, u32[]{:S(2)}, u32[]{:S(2)}) collective-permute-start(bf16[2,4096,128]{2,1,0:T(8,128)(2,1)} %bitcast.40), channel_id=1, source_target_pairs={{0,8},{8,0},{16,24},{24,16},{32,40},{40,32},{48,56},{56,48},{64,72... | collective-permute-start | bytes 6291464 | tf_op jit(solution)/shard_map/ppermute | solution.py:335
  7.8 34.5 %copy-start = (bf16[256,1024]{1,0:T(8,128)(2,1)S(1)}, bf16[256,1024]{1,0:T(8,128)(2,1)}, u32[]{:S(2)}) copy-start(bf16[256,1024]{1,0:T(8,128)(2,1)} %q_ref.9) | copy-start | bytes 1572868
  7.9 7.5 %collective-permute-start.28 = (bf16[2,512,128]{2,1,0:T(8,128)(2,1)S(1)}, bf16[2,512,128]{2,1,0:T(8,128)(2,1)S(1)}, u32[]{:S(2)}, u32[]{:S(2)}) collective-permute-start(bf16[2,512,128]{2,1,0:T(8,128)(2,1)S(1)} %get-tuple-element.154), channel_id=1, source_target_pairs={{16,32},{24,8},{48,64},{56,40},{80,96},{88,72},{112,0},{120,104},{... | collective-permute-start | bytes 786440 | tf_op jit(solution)/shard_map/cond/branch_7_fun/ppermute | solution.py:350
  9.4 6.1 %collective-permute-start.29 = (bf16[2,512,128]{2,1,0:T(8,128)(2,1)S(1)}, bf16[2,512,128]{2,1,0:T(8,128)(2,1)S(1)}, u32[]{:S(2)}, u32[]{:S(2)}) collective-permute-start(bf16[2,512,128]{2,1,0:T(8,128)(2,1)S(1)} %get-tuple-element.155), channel_id=1, source_target_pairs={{48,80},{56,24},{112,16},{120,88},{176,208},{184,152},{240,144},{2... | collective-permute-start | bytes 786440 | tf_op jit(solution)/shard_map/cond/branch_7_fun/ppermute | solution.py:350
  10.0 5.4 %collective-permute-start.30 = (bf16[2,512,128]{2,1,0:T(8,128)(2,1)S(1)}, bf16[2,512,128]{2,1,0:T(8,128)(2,1)S(1)}, u32[]{:S(2)}, u32[]{:S(2)}) collective-permute-start(bf16[2,512,128]{2,1,0:T(8,128)(2,1)S(1)} %get-tuple-element.156), channel_id=1, source_target_pairs={{112,32},{120,72},{240,160},{248,200},{113,33},{121,73},{241,161},... | collective-permute-start | bytes 786440 | tf_op jit(solution)/shard_map/cond/branch_7_fun/ppermute | solution.py:350
  10.7 0.7 collective-permute-start.31
  15.7 3.8 %collective-permute-start.33 = (bf16[2,256,128]{2,1,0:T(8,128)(2,1)S(1)}, bf16[2,256,128]{2,1,0:T(8,128)(2,1)S(1)}, u32[]{:S(2)}, u32[]{:S(2)}) collective-permute-start(bf16[2,256,128]{2,1,0:T(8,128)(2,1)S(1)} %constant_dynamic-slice_fusion), channel_id=1, source_target_pairs={{0,8},{8,0},{16,24},{24,16},{32,40},{40,32},{48,56},{56,48},{64,72... | collective-permute-start | bytes 393224 | tf_op jit(solution)/shard_map/ppermute | solution.py:359
  19.5 6.3 %collective-permute-start.34 = (bf16[2,256,128]{2,1,0:T(8,128)(2,1)S(1)}, bf16[2,256,128]{2,1,0:T(8,128)(2,1)S(1)}, u32[]{:S(2)}, u32[]{:S(2)}) collective-permute-start(bf16[2,256,128]{2,1,0:T(8,128)(2,1)S(1)} %dynamic-slice_select_fusion), channel_id=1, source_target_pairs={{0,128},{8,136},{16,144},{24,152},{32,160},{40,168},{48,176},{56,1... | collective-permute-start | bytes 393224 | tf_op jit(solution)/shard_map/ppermute | solution.py:361
  25.8 16.5 %collective-permute-start.38 = (bf16[1,2,256,128]{3,2,1,0:T(8,128)(2,1)S(1)}, bf16[1,2,256,128]{3,2,1,0:T(8,128)(2,1)S(1)}, u32[]{:S(2)}, u32[]{:S(2)}) collective-permute-start(bf16[1,2,256,128]{3,2,1,0:T(8,128)(2,1)S(1)} %select_bitcast_fusion.refs_0_), channel_id=1, source_target_pairs={{0,8},{8,0},{16,24},{24,16},{32,40},{40,32},{48,56},{56,48},{64,72... | collective-permute-start | bytes 393224 | tf_op jit(solution)/shard_map/ppermute | solution.py:367
  27.1 19.6 %collective-permute-start.35 = (bf16[1,2,256,128]{3,2,1,0:T(8,128)(2,1)S(1)}, bf16[1,2,256,128]{3,2,1,0:T(8,128)(2,1)S(1)}, u32[]{:S(2)}, u32[]{:S(2)}) collective-permute-start(bf16[1,2,256,128]{3,2,1,0:T(8,128)(2,1)S(1)} %select_bitcast_fusion.refs_0_), channel_id=1, source_target_pairs={{0,112},{8,120},{16,0},{24,8},{32,16},{40,24},{48,32},{56,40},{64,... | collective-permute-start | bytes 393224 | tf_op jit(solution)/shard_map/ppermute | solution.py:365
  36.2 10.5 %collective-permute-start.36 = (bf16[1,2,256,128]{3,2,1,0:T(8,128)(2,1)S(1)}, bf16[1,2,256,128]{3,2,1,0:T(8,128)(2,1)S(1)}, u32[]{:S(2)}, u32[]{:S(2)}) collective-permute-start(bf16[1,2,256,128]{3,2,1,0:T(8,128)(2,1)S(1)} %select_bitcast_fusion.refs_0_), channel_id=1, source_target_pairs={{0,16},{8,24},{16,32},{24,40},{32,48},{40,56},{48,64},{56,72},{64,... | collective-permute-start | bytes 393224 | tf_op jit(solution)/shard_map/ppermute | solution.py:366
  36.2 15.2 %collective-permute-start.37 = (bf16[1,2,256,128]{3,2,1,0:T(8,128)(2,1)S(1)}, bf16[1,2,256,128]{3,2,1,0:T(8,128)(2,1)S(1)}, u32[]{:S(2)}, u32[]{:S(2)}) collective-permute-start(bf16[1,2,256,128]{3,2,1,0:T(8,128)(2,1)S(1)} %select_bitcast_fusion.refs_0_), channel_id=1, source_target_pairs={{0,64},{8,72},{16,80},{24,88},{32,96},{40,104},{48,112},{56,120},{... | collective-permute-start | bytes 393224 | tf_op jit(solution)/shard_map/ppermute | solution.py:364
  51.5 5.7 %collective-permute-start.41 = (bf16[3,2,256,128]{3,2,1,0:T(8,128)(2,1)S(1)}, bf16[3,2,256,128]{3,2,1,0:T(8,128)(2,1)S(1)}, u32[]{:S(2)}, u32[]{:S(2)}) collective-permute-start(bf16[3,2,256,128]{3,2,1,0:T(8,128)(2,1)S(1)} %pad_maximum_fusion.1), channel_id=1, source_target_pairs={{0,8},{8,0},{16,24},{24,16},{32,40},{40,32},{48,56},{56,48},{64,72... | collective-permute-start | bytes 1179656 | tf_op jit(solution)/shard_map/ppermute | solution.py:373
  52.6 7.9 %collective-permute-start.39 = (bf16[2,2,256,128]{3,2,1,0:T(8,128)(2,1)S(1)}, bf16[2,2,256,128]{3,2,1,0:T(8,128)(2,1)S(1)}, u32[]{:S(2)}, u32[]{:S(2)}) collective-permute-start(bf16[2,2,256,128]{3,2,1,0:T(8,128)(2,1)S(1)} %get-tuple-element.246), channel_id=1, source_target_pairs={{0,112},{8,120},{16,0},{24,8},{32,16},{40,24},{48,32},{56,40},{64,... | collective-permute-start | bytes 786440 | tf_op jit(solution)/shard_map/ppermute | solution.py:371
  52.7 9.3 %collective-permute-start.40 = (bf16[2,2,256,128]{3,2,1,0:T(8,128)(2,1)S(1)}, bf16[2,2,256,128]{3,2,1,0:T(8,128)(2,1)S(1)}, u32[]{:S(2)}, u32[]{:S(2)}) collective-permute-start(bf16[2,2,256,128]{3,2,1,0:T(8,128)(2,1)S(1)} %get-tuple-element.245), channel_id=1, source_target_pairs={{0,16},{8,24},{16,32},{24,40},{32,48},{40,56},{48,64},{56,72},{64,... | collective-permute-start | bytes 786440 | tf_op jit(solution)/shard_map/ppermute | solution.py:372
  62.0 4.7 %collective-permute-start.42 = (bf16[4,2,256,128]{3,2,1,0:T(8,128)(2,1)S(1)}, bf16[4,2,256,128]{3,2,1,0:T(8,128)(2,1)S(1)}, u32[]{:S(2)}, u32[]{:S(2)}) collective-permute-start(bf16[4,2,256,128]{3,2,1,0:T(8,128)(2,1)S(1)} %pad_maximum_fusion), channel_id=1, source_target_pairs={{0,8},{8,0},{16,24},{24,16},{32,40},{40,32},{48,56},{56,48},{64,72... | collective-permute-start | bytes 1572872 | tf_op jit(solution)/shard_map/ppermute | solution.py:378
  73.3 9.1 %collective-permute-start.43 = (bf16[2,32,2048]{2,1,0:T(8,128)(2,1)S(1)}, bf16[2,32,2048]{2,1,0:T(8,128)(2,1)S(1)}, u32[]{:S(2)}, u32[]{:S(2)}) collective-permute-start(bf16[2,32,2048]{2,1,0:T(8,128)(2,1)S(1)} %get-tuple-element.235), channel_id=1, source_target_pairs={{0,1},{1,2},{2,3},{3,0},{4,5},{5,6},{6,7},{7,4},{8,9},{9,10},{10,1... | collective-permute-start | bytes 786440 | tf_op jit(solution)/shard_map/ppermute | solution.py:305
  74.6 7.9 %collective-permute-start.44 = (bf16[2,32,2048]{2,1,0:T(8,128)(2,1)S(1)}, bf16[2,32,2048]{2,1,0:T(8,128)(2,1)S(1)}, u32[]{:S(2)}, u32[]{:S(2)}) collective-permute-start(bf16[2,32,2048]{2,1,0:T(8,128)(2,1)S(1)} %get-tuple-element.236), channel_id=1, source_target_pairs={{0,3},{1,0},{2,1},{3,2},{4,7},{5,4},{6,5},{7,6},{8,11},{9,8},{10,9... | collective-permute-start | bytes 786440 | tf_op jit(solution)/shard_map/ppermute | solution.py:306
  76.0 13.0 %collective-permute-start.45 = (bf16[2,32,2048]{2,1,0:T(8,128)(2,1)S(1)}, bf16[2,32,2048]{2,1,0:T(8,128)(2,1)S(1)}, u32[]{:S(2)}, u32[]{:S(2)}) collective-permute-start(bf16[2,32,2048]{2,1,0:T(8,128)(2,1)S(1)} %get-tuple-element.237), channel_id=1, source_target_pairs={{0,2},{1,3},{2,0},{3,1},{4,6},{5,7},{6,4},{7,5},{8,10},{9,11},{10,... | collective-permute-start | bytes 786440 | tf_op jit(solution)/shard_map/ppermute | solution.py:304
  77.6 13.0 %collective-permute-start.47 = (bf16[4,32,2048]{2,1,0:T(8,128)(2,1)S(1)}, bf16[4,32,2048]{2,1,0:T(8,128)(2,1)S(1)}, u32[]{:S(2)}, u32[]{:S(2)}) collective-permute-start(bf16[4,32,2048]{2,1,0:T(8,128)(2,1)S(1)} %get-tuple-element.239), channel_id=1, source_target_pairs={{0,4},{1,5},{2,6},{3,7},{4,0},{5,1},{6,2},{7,3},{8,12},{9,13},{10,... | collective-permute-start | bytes 1572872 | tf_op jit(solution)/shard_map/ppermute | solution.py:302
  89.2 4.3 %collective-permute-start.46 = (bf16[32,2048]{1,0:T(8,128)(2,1)S(1)}, bf16[32,2048]{1,0:T(8,128)(2,1)S(1)}, u32[]{:S(2)}, u32[]{:S(2)}) collective-permute-start(bf16[32,2048]{1,0:T(8,128)(2,1)S(1)} %fusion.22), channel_id=1, source_target_pairs={{0,4},{1,5},{2,6},{3,7},{4,0},{5,1},{6,2},{7,3},{8,12},{9,13},{10,... | collective-permute-start | bytes 393224 | tf_op jit(solution)/shard_map/ppermute | solution.py:313
  90.7 5.1 %collective-permute-start.48 = (bf16[32,2048]{1,0:T(8,128)(2,1)S(1)}, bf16[32,2048]{1,0:T(8,128)(2,1)S(1)}, u32[]{:S(2)}, u32[]{:S(2)}) collective-permute-start(bf16[32,2048]{1,0:T(8,128)(2,1)S(1)} %get-tuple-element.242), channel_id=1, source_target_pairs={{0,1},{1,2},{2,3},{3,0},{4,5},{5,6},{6,7},{7,4},{8,9},{9,10},{10,1... | collective-permute-start | bytes 393224 | tf_op jit(solution)/shard_map/ppermute | solution.py:309
  91.4 5.8 %collective-permute-start.49 = (bf16[32,2048]{1,0:T(8,128)(2,1)S(1)}, bf16[32,2048]{1,0:T(8,128)(2,1)S(1)}, u32[]{:S(2)}, u32[]{:S(2)}) collective-permute-start(bf16[32,2048]{1,0:T(8,128)(2,1)S(1)} %get-tuple-element.244), channel_id=1, source_target_pairs={{0,3},{1,0},{2,1},{3,2},{4,7},{5,4},{6,5},{7,6},{8,11},{9,8},{10,9... | collective-permute-start | bytes 393224 | tf_op jit(solution)/shard_map/ppermute | solution.py:310
  93.5 5.6 %collective-permute-start.50 = (bf16[32,2048]{1,0:T(8,128)(2,1)S(1)}, bf16[32,2048]{1,0:T(8,128)(2,1)S(1)}, u32[]{:S(2)}, u32[]{:S(2)}) collective-permute-start(bf16[32,2048]{1,0:T(8,128)(2,1)S(1)} %get-tuple-element.243), channel_id=1, source_target_pairs={{0,2},{1,3},{2,0},{3,1},{4,6},{5,7},{6,4},{7,5},{8,10},{9,11},{10,... | collective-permute-start | bytes 393224 | tf_op jit(solution)/shard_map/ppermute | solution.py:311
  (6 other events, 139.0 us)

commit v3 on v2

--- a/solution.py
+++ b/solution.py
@@ -189,9 +189,9 @@
 def windows(at):
     z, c = at[1], at[2]
     up = 1 - 2 * c
-    spots = [(z * 2 * PIECE + c * PIECE, PIECE)]
-    spots += [(lax.rem(z + up * d + 8, 8) * 2 * PIECE, 2 * PIECE) for d in (1, 2, 3)]
-    spots.append((lax.rem(z + 4, 8) * 2 * PIECE + c * PIECE, PIECE))
+    ahead = lambda d: (lax.rem(z + up * d + 8, 8) * 2 * PIECE, 2 * PIECE)
+    half = lambda d: (lax.rem(z + d, 8) * 2 * PIECE + c * PIECE, PIECE)
+    spots = [ahead(3), half(4), ahead(2), ahead(1), half(0)]
     return [pl.ds(pl.multiple_of(start, PIECE), size) for start, size in spots]
 
 
@@ -225,7 +225,7 @@
     part = lambda size: jax.ShapeDtypeStruct((2, size, HD), jnp.bfloat16)
     return pl.pallas_call(
         kernel,
-        out_shape=(part(PIECE),) + (part(2 * PIECE),) * 3 + (part(PIECE),),
+        out_shape=tuple(part(n * PIECE) for n in (2, 1, 2, 2, 1)),
         in_specs=[SM] + [VM if mine else ANY] * (1 + len(mine)),
         out_specs=(VM,) * 5,
         scratch_shapes=[] if mine else [pltpu.SemaphoreType.DMA((5,))],
@@ -334,7 +334,7 @@
     )
     partner = over_rep(prefix, perm=CORE_SWAP)
     parts = cut_call(cut_kernel, cut_at, prefix)
-    own, *outgoing = cut_call(choose_kernel, cut_at, partner, *parts)
+    part_3, part_4, part_2, part_1, own = cut_call(choose_kernel, cut_at, partner, *parts)
 
     def branch(b):
         def send(steps, own, *parts):
@@ -354,7 +354,7 @@
 
         return send
 
-    slot = lax.switch(root_z, [branch(b) for b in range(8)], steps, own, *outgoing)
+    slot = lax.switch(root_z, [branch(b) for b in range(8)], steps, own, part_1, part_2, part_3, part_4)
     half_of = lambda a, c: lax.dynamic_slice_in_dim(a, c * PIECE, PIECE, 1)
     from_partner = over_rep(half_of(slot, 1 - my_c), perm=CORE_SWAP)
     piece = jnp.where(steps <= 4, half_of(slot, my_c), from_partner)

time: 101 us -> 101 us (level)
  no operation moved by 1% of the time
where the time goes in v3:
time: 101 us; the launch traced here: 99.9 us
  starting transfers between devices  42.2 us (42%)
  waiting for transfers between devices  31.1 us (31%)
  Pallas kernels  22 us (22%)
  local copies, waits for them, and re-layouts  1.7 us (2%)
  other arithmetic  1.6 us (2%)
  between operations  1.08 us (1%)
    pallas_call x3, Pallas kernels, mid_call(): pl.pallas_call(functools.partial(mid_kernel, n), out_shape=state_shapes(r...  9.78 us
    ppermute x1, starting transfers between devices, body(): above = over_rep(a0, perm=z_shift(-1))  9.1 us
    ppermute x1, waiting for transfers between devices, reduce_rows(): r2 = over_tp(x2, perm=x_shift(2))  6.6 us
    ppermute x1, starting transfers between devices, body(): facing = over_rep(a0, perm=z_shift(4))  6.07 us
    pallas_call x1, Pallas kernels, last_call(): pl.pallas_call(functools.partial(last_kernel, n), out_shape=outs, in_spec...  5.01 us
    ppermute x1, waiting for transfers between devices, body(): facing = over_rep(a0, perm=z_shift(4))  4.68 us
    pallas_call x1, Pallas kernels, first_call(): pl.pallas_call(first_kernel, out_shape=state_shapes(rows), in_specs=[SM]...  4.35 us
    ppermute x4, waiting for transfers between devices, send(): got[d] = over_rep(parts[d - 1], perm=pairs)  4.05 us
  transfers between devices with their start and end apart: 23, of which 12 were waited for; matrix products, arithmetic and copies ran while one was open for 1% of the time, Pallas kernels for 15%

profile of v3, /device:TPU:1, one launch (start us, length us, event | category | flops | bytes accessed | tf_op | source)
XLA Modules:
  0.0 99.9 jit_solution(9296594409787374402)
XLA Ops:
  0.0 3.2 %collective-permute-start.32 = (bf16[2,4096,128]{2,1,0:T(8,128)(2,1)}, bf16[2,4096,128]{2,1,0:T(8,128)(2,1)S(1)}, u32[]{:S(2)}, u32[]{:S(2)}) collective-permute-start(bf16[2,4096,128]{2,1,0:T(8,128)(2,1)} %bitcast.40), channel_id=1, source_target_pairs={{0,8},{8,0},{16,24},{24,16},{32,40},{40,32},{48,56},{56,48},{64,72... | collective-permute-start | bytes 6291464 | tf_op jit(solution)/shard_map/ppermute | solution.py:335
  4.2 1.6 %copy-done.1 = bf16[1,2,4096,128]{3,2,1,0:T(8,128)(2,1)S(1)} copy-done((bf16[1,2,4096,128]{3,2,1,0:T(8,128)(2,1)S(1)}, bf16[1,2,4096,128]{3,2,1,0:T(8,128)(2,1)}, u32[]{:S(2)}) %copy-start.1) | copy-done | bytes 2097176
  7.9 7.8 %conditional.1 = (bf16[2,512,128]{2,1,0:T(8,128)(2,1)S(1)}) conditional(s32[]{:T(128)} %clamp.3, (s32[]{:T(128)}, bf16[2,256,128]{2,1,0:T(8,128)(2,1)S(1)}, bf16[2,512,128]{2,1,0:T(8,128)(2,1)S(1)}, bf16[2,512,128]{2,1,0:T(8,128)(2,1)S(1)}, bf16[2,512,128]{2,1,0:T(8,128)(2,1)S(1)}, ...), branch_computations={%region_0.1_spmd, %region_1.2_spmd, %region_2.3_spmd, %region_3.4_... | conditional | flops 1572869 | bytes 4980956 | solution.py:357
  11.4 4.0 %collective-permute-done.28 = bf16[2,512,128]{2,1,0:T(8,128)(2,1)S(1)} collective-permute-done((bf16[2,512,128]{2,1,0:T(8,128)(2,1)S(1)}, bf16[2,512,128]{2,1,0:T(8,128)(2,1)S(1)}, u32[]{:S(2)}, u32[]{:S(2)}) %collective-permute-start.28) | collective-permute-done | bytes 262176 | tf_op jit(solution)/shard_map/cond/branch_7_fun/ppermute | solution.py:350
  15.7 2.8 %collective-permute-start.33 = (bf16[2,256,128]{2,1,0:T(8,128)(2,1)S(1)}, bf16[2,256,128]{2,1,0:T(8,128)(2,1)S(1)}, u32[]{:S(2)}, u32[]{:S(2)}) collective-permute-start(bf16[2,256,128]{2,1,0:T(8,128)(2,1)S(1)} %constant_dynamic-slice_fusion), channel_id=1, source_target_pairs={{0,8},{8,0},{16,24},{24,16},{32,40},{40,32},{48,56},{56,48},{64,72... | collective-permute-start | bytes 393224 | tf_op jit(solution)/shard_map/ppermute | solution.py:359
  19.5 3.0 %collective-permute-start.34 = (bf16[2,256,128]{2,1,0:T(8,128)(2,1)S(1)}, bf16[2,256,128]{2,1,0:T(8,128)(2,1)S(1)}, u32[]{:S(2)}, u32[]{:S(2)}) collective-permute-start(bf16[2,256,128]{2,1,0:T(8,128)(2,1)S(1)} %dynamic-slice_select_fusion), channel_id=1, source_target_pairs={{0,128},{8,136},{16,144},{24,152},{32,160},{40,168},{48,176},{56,1... | collective-permute-start | bytes 393224 | tf_op jit(solution)/shard_map/ppermute | solution.py:361
  22.5 3.3 %collective-permute-done.34 = bf16[2,256,128]{2,1,0:T(8,128)(2,1)S(1)} collective-permute-done((bf16[2,256,128]{2,1,0:T(8,128)(2,1)S(1)}, bf16[2,256,128]{2,1,0:T(8,128)(2,1)S(1)}, u32[]{:S(2)}, u32[]{:S(2)}) %collective-permute-start.34) | collective-permute-done | bytes 131104 | tf_op jit(solution)/shard_map/ppermute | solution.py:361
  27.1 9.1 %collective-permute-start.35 = (bf16[1,2,256,128]{3,2,1,0:T(8,128)(2,1)S(1)}, bf16[1,2,256,128]{3,2,1,0:T(8,128)(2,1)S(1)}, u32[]{:S(2)}, u32[]{:S(2)}) collective-permute-start(bf16[1,2,256,128]{3,2,1,0:T(8,128)(2,1)S(1)} %select_bitcast_fusion.refs_0_), channel_id=1, source_target_pairs={{0,112},{8,120},{16,0},{24,8},{32,16},{40,24},{48,32},{56,40},{64,... | collective-permute-start | bytes 393224 | tf_op jit(solution)/shard_map/ppermute | solution.py:365
  36.2 6.1 %collective-permute-start.37 = (bf16[1,2,256,128]{3,2,1,0:T(8,128)(2,1)S(1)}, bf16[1,2,256,128]{3,2,1,0:T(8,128)(2,1)S(1)}, u32[]{:S(2)}, u32[]{:S(2)}) collective-permute-start(bf16[1,2,256,128]{3,2,1,0:T(8,128)(2,1)S(1)} %select_bitcast_fusion.refs_0_), channel_id=1, source_target_pairs={{0,64},{8,72},{16,80},{24,88},{32,96},{40,104},{48,112},{56,120},{... | collective-permute-start | bytes 393224 | tf_op jit(solution)/shard_map/ppermute | solution.py:364
  42.4 4.3 %attn_first.1 = (f32[8,256,128]{2,1,0:T(8,128)S(1)}, f32[8,256,256]{2,1,0:T(8,128)S(1)}) custom-call(s32[2]{0:T(128)S(1)} %bitcast.42, bf16[256,1024]{1,0:T(8,128)(2,1)S(1)} %copy-done, bf16[256,128]{1,0:T(8,128)(2,1)S(1)} %copy-done.2, bf16[256,128]{1,0:T(8,128)(2,1)S(1)} %copy-done.3, bf16[1,2,256,128]{3,2,1,0:T(8,128)(2,1)S(1)} %select_bitcast_fusion.refs_0_, ...), custom_call_target="tpu_custom_call" | custom-call | flops 805306368 | tf_op jit(solution)/shard_map/attn_first/pallas_call | solution.py:239
  46.7 4.7 %collective-permute-done.37.refs_2_ = bf16[1,2,256,128]{3,2,1,0:T(8,128)(2,1)S(1)} collective-permute-done((bf16[1,2,256,128]{3,2,1,0:T(8,128)(2,1)S(1)}, bf16[1,2,256,128]{3,2,1,0:T(8,128)(2,1)S(1)}, u32[]{:S(2)}, u32[]{:S(2)}) %collective-permute-start.37) | collective-permute-done | bytes 131104 | tf_op jit(solution)/shard_map/ppermute | solution.py:364
  52.7 1.5 %collective-permute-start.40 = (bf16[2,2,256,128]{3,2,1,0:T(8,128)(2,1)S(1)}, bf16[2,2,256,128]{3,2,1,0:T(8,128)(2,1)S(1)}, u32[]{:S(2)}, u32[]{:S(2)}) collective-permute-start(bf16[2,2,256,128]{3,2,1,0:T(8,128)(2,1)S(1)} %get-tuple-element.245), channel_id=1, source_target_pairs={{0,16},{8,24},{16,32},{24,40},{32,48},{40,56},{48,64},{56,72},{64,... | collective-permute-start | bytes 786440 | tf_op jit(solution)/shard_map/ppermute | solution.py:372
  54.1 3.1 %attn_mid.3 = (f32[8,256,128]{2,1,0:T(8,128)S(1)}, f32[8,256,256]{2,1,0:T(8,128)S(1)}) custom-call(bf16[256,1024]{1,0:T(8,128)(2,1)S(1)} %copy-done, bf16[1,2,256,128]{3,2,1,0:T(8,128)(2,1)S(1)} %collective-permute-done.35.refs_0_, bf16[1,2,256,128]{3,2,1,0:T(8,128)(2,1)S(1)} %collective-permute-done.36.refs_1_, ...), custom_call_target="tpu_custom_call", output_to_operand_aliasing={{0}: (4, {}), {1}: (5, {})} | custom-call | flops 805306368 | tf_op jit(solution)/shard_map/attn_mid/pallas_call | solution.py:253
  57.2 3.0 %attn_mid.4 = (f32[8,256,128]{2,1,0:T(8,128)S(1)}, f32[8,256,256]{2,1,0:T(8,128)S(1)}) custom-call(bf16[256,1024]{1,0:T(8,128)(2,1)S(1)} %copy-done, bf16[3,2,256,128]{3,2,1,0:T(8,128)(2,1)S(1)} %collective-permute-done.41.refs_0_, f32[8,256,128]{2,1,0:T(8,128)S(1)} %get-tuple-element.223.refs_1_, ...), custom_call_target="tpu_custom_call", output_to_operand_aliasing={{0}: (2, {}), {1}: (3, {})} | custom-call | flops 805306368 | tf_op jit(solution)/shard_map/attn_mid/pallas_call | solution.py:253
  60.5 1.5 %collective-permute-done.40.refs_1_ = bf16[2,2,256,128]{3,2,1,0:T(8,128)(2,1)S(1)} collective-permute-done((bf16[2,2,256,128]{3,2,1,0:T(8,128)(2,1)S(1)}, bf16[2,2,256,128]{3,2,1,0:T(8,128)(2,1)S(1)}, u32[]{:S(2)}, u32[]{:S(2)}) %collective-permute-start.40) | collective-permute-done | bytes 262176 | tf_op jit(solution)/shard_map/ppermute | solution.py:372
  63.0 3.8 %attn_mid.5 = (f32[8,256,128]{2,1,0:T(8,128)S(1)}, f32[8,256,256]{2,1,0:T(8,128)S(1)}) custom-call(bf16[256,1024]{1,0:T(8,128)(2,1)S(1)} %copy-done, bf16[2,2,256,128]{3,2,1,0:T(8,128)(2,1)S(1)} %collective-permute-done.39.refs_0_, bf16[2,2,256,128]{3,2,1,0:T(8,128)(2,1)S(1)} %collective-permute-done.40.refs_1_, ...), custom_call_target="tpu_custom_call", output_to_operand_aliasing={{0}: (3, {}), {1}: (4, {})} | custom-call | flops 1073741824 | tf_op jit(solution)/shard_map/attn_mid/pallas_call | solution.py:253
  66.8 5.0 %attn_last.1 = (bf16[256,1024]{1,0:T(8,128)(2,1)S(1)}, bf16[4,32,2048]{2,1,0:T(8,128)(2,1)S(1)}, bf16[4,32,2048]{2,1,0:T(8,128)(2,1)S(1)}) custom-call(s32[2]{0:T(128)S(1)} %pad_add_fusion.1.spot, bf16[256,1024]{1,0:T(8,128)(2,1)S(1)} %copy-done, bf16[4,2,256,128]{3,2,1,0:T(8,128)(2,1)S(1)} %collective-permute-done.42.refs_0_, ...), custom_call_target="tpu_custom_call" | custom-call | flops 2147483648 | tf_op jit(solution)/shard_map/attn_last/pallas_call | solution.py:270
  74.6 1.5 %collective-permute-start.44 = (bf16[2,32,2048]{2,1,0:T(8,128)(2,1)S(1)}, bf16[2,32,2048]{2,1,0:T(8,128)(2,1)S(1)}, u32[]{:S(2)}, u32[]{:S(2)}) collective-permute-start(bf16[2,32,2048]{2,1,0:T(8,128)(2,1)S(1)} %get-tuple-element.236), channel_id=1, source_target_pairs={{0,3},{1,0},{2,1},{3,2},{4,7},{5,4},{6,5},{7,6},{8,11},{9,8},{10,9... | collective-permute-start | bytes 786440 | tf_op jit(solution)/shard_map/ppermute | solution.py:306
  76.0 1.5 %collective-permute-start.45 = (bf16[2,32,2048]{2,1,0:T(8,128)(2,1)S(1)}, bf16[2,32,2048]{2,1,0:T(8,128)(2,1)S(1)}, u32[]{:S(2)}, u32[]{:S(2)}) collective-permute-start(bf16[2,32,2048]{2,1,0:T(8,128)(2,1)S(1)} %get-tuple-element.237), channel_id=1, source_target_pairs={{0,2},{1,3},{2,0},{3,1},{4,6},{5,7},{6,4},{7,5},{8,10},{9,11},{10,... | collective-permute-start | bytes 786440 | tf_op jit(solution)/shard_map/ppermute | solution.py:304
  78.8 3.6 %collective-permute-done.43 = bf16[2,32,2048]{2,1,0:T(8,128)(2,1)S(1)} collective-permute-done((bf16[2,32,2048]{2,1,0:T(8,128)(2,1)S(1)}, bf16[2,32,2048]{2,1,0:T(8,128)(2,1)S(1)}, u32[]{:S(2)}, u32[]{:S(2)}) %collective-permute-start.43) | collective-permute-done | bytes 262176 | tf_op jit(solution)/shard_map/ppermute | solution.py:305
  82.4 6.6 %collective-permute-done.45 = bf16[2,32,2048]{2,1,0:T(8,128)(2,1)S(1)} collective-permute-done((bf16[2,32,2048]{2,1,0:T(8,128)(2,1)S(1)}, bf16[2,32,2048]{2,1,0:T(8,128)(2,1)S(1)}, u32[]{:S(2)}, u32[]{:S(2)}) %collective-permute-start.45) | collective-permute-done | bytes 262176 | tf_op jit(solution)/shard_map/ppermute | solution.py:304
  91.4 2.1 %collective-permute-start.49 = (bf16[32,2048]{1,0:T(8,128)(2,1)S(1)}, bf16[32,2048]{1,0:T(8,128)(2,1)S(1)}, u32[]{:S(2)}, u32[]{:S(2)}) collective-permute-start(bf16[32,2048]{1,0:T(8,128)(2,1)S(1)} %get-tuple-element.244), channel_id=1, source_target_pairs={{0,3},{1,0},{2,1},{3,2},{4,7},{5,4},{6,5},{7,6},{8,11},{9,8},{10,9... | collective-permute-start | bytes 393224 | tf_op jit(solution)/shard_map/ppermute | solution.py:310
  93.5 2.3 %collective-permute-done.48 = bf16[32,2048]{1,0:T(8,128)(2,1)S(1)} collective-permute-done((bf16[32,2048]{1,0:T(8,128)(2,1)S(1)}, bf16[32,2048]{1,0:T(8,128)(2,1)S(1)}, u32[]{:S(2)}, u32[]{:S(2)}) %collective-permute-start.48) | collective-permute-done | bytes 131104 | tf_op jit(solution)/shard_map/ppermute | solution.py:309
  97.2 1.9 %collective-permute-done.50 = bf16[32,2048]{1,0:T(8,128)(2,1)S(1)} collective-permute-done((bf16[32,2048]{1,0:T(8,128)(2,1)S(1)}, bf16[32,2048]{1,0:T(8,128)(2,1)S(1)}, u32[]{:S(2)}, u32[]{:S(2)}) %collective-permute-start.50) | collective-permute-done | bytes 131104 | tf_op jit(solution)/shard_map/ppermute | solution.py:311
  (62 shorter events, 19.4 us)
Async XLA Ops:
  0.0 7.2 %collective-permute-start.32 = (bf16[2,4096,128]{2,1,0:T(8,128)(2,1)}, bf16[2,4096,128]{2,1,0:T(8,128)(2,1)S(1)}, u32[]{:S(2)}, u32[]{:S(2)}) collective-permute-start(bf16[2,4096,128]{2,1,0:T(8,128)(2,1)} %bitcast.40), channel_id=1, source_target_pairs={{0,8},{8,0},{16,24},{24,16},{32,40},{40,32},{48,56},{56,48},{64,72... | collective-permute-start | bytes 6291464 | tf_op jit(solution)/shard_map/ppermute | solution.py:335
  7.8 34.5 %copy-start = (bf16[256,1024]{1,0:T(8,128)(2,1)S(1)}, bf16[256,1024]{1,0:T(8,128)(2,1)}, u32[]{:S(2)}) copy-start(bf16[256,1024]{1,0:T(8,128)(2,1)} %q_ref.9) | copy-start | bytes 1572868
  7.9 7.5 %collective-permute-start.28 = (bf16[2,512,128]{2,1,0:T(8,128)(2,1)S(1)}, bf16[2,512,128]{2,1,0:T(8,128)(2,1)S(1)}, u32[]{:S(2)}, u32[]{:S(2)}) collective-permute-start(bf16[2,512,128]{2,1,0:T(8,128)(2,1)S(1)} %get-tuple-element.154), channel_id=1, source_target_pairs={{16,32},{24,8},{48,64},{56,40},{80,96},{88,72},{112,0},{120,104},{... | collective-permute-start | bytes 786440 | tf_op jit(solution)/shard_map/cond/branch_7_fun/ppermute | solution.py:350
  9.4 6.1 %collective-permute-start.29 = (bf16[2,512,128]{2,1,0:T(8,128)(2,1)S(1)}, bf16[2,512,128]{2,1,0:T(8,128)(2,1)S(1)}, u32[]{:S(2)}, u32[]{:S(2)}) collective-permute-start(bf16[2,512,128]{2,1,0:T(8,128)(2,1)S(1)} %get-tuple-element.155), channel_id=1, source_target_pairs={{48,80},{56,24},{112,16},{120,88},{176,208},{184,152},{240,144},{2... | collective-permute-start | bytes 786440 | tf_op jit(solution)/shard_map/cond/branch_7_fun/ppermute | solution.py:350
  10.1 5.4 %collective-permute-start.30 = (bf16[2,512,128]{2,1,0:T(8,128)(2,1)S(1)}, bf16[2,512,128]{2,1,0:T(8,128)(2,1)S(1)}, u32[]{:S(2)}, u32[]{:S(2)}) collective-permute-start(bf16[2,512,128]{2,1,0:T(8,128)(2,1)S(1)} %get-tuple-element.156), channel_id=1, source_target_pairs={{112,32},{120,72},{240,160},{248,200},{113,33},{121,73},{241,161},... | collective-permute-start | bytes 786440 | tf_op jit(solution)/shard_map/cond/branch_7_fun/ppermute | solution.py:350
  10.7 0.7 collective-permute-start.31
  15.7 3.8 %collective-permute-start.33 = (bf16[2,256,128]{2,1,0:T(8,128)(2,1)S(1)}, bf16[2,256,128]{2,1,0:T(8,128)(2,1)S(1)}, u32[]{:S(2)}, u32[]{:S(2)}) collective-permute-start(bf16[2,256,128]{2,1,0:T(8,128)(2,1)S(1)} %constant_dynamic-slice_fusion), channel_id=1, source_target_pairs={{0,8},{8,0},{16,24},{24,16},{32,40},{40,32},{48,56},{56,48},{64,72... | collective-permute-start | bytes 393224 | tf_op jit(solution)/shard_map/ppermute | solution.py:359
  19.5 6.3 %collective-permute-start.34 = (bf16[2,256,128]{2,1,0:T(8,128)(2,1)S(1)}, bf16[2,256,128]{2,1,0:T(8,128)(2,1)S(1)}, u32[]{:S(2)}, u32[]{:S(2)}) collective-permute-start(bf16[2,256,128]{2,1,0:T(8,128)(2,1)S(1)} %dynamic-slice_select_fusion), channel_id=1, source_target_pairs={{0,128},{8,136},{16,144},{24,152},{32,160},{40,168},{48,176},{56,1... | collective-permute-start | bytes 393224 | tf_op jit(solution)/shard_map/ppermute | solution.py:361
  25.8 16.5 %collective-permute-start.38 = (bf16[1,2,256,128]{3,2,1,0:T(8,128)(2,1)S(1)}, bf16[1,2,256,128]{3,2,1,0:T(8,128)(2,1)S(1)}, u32[]{:S(2)}, u32[]{:S(2)}) collective-permute-start(bf16[1,2,256,128]{3,2,1,0:T(8,128)(2,1)S(1)} %select_bitcast_fusion.refs_0_), channel_id=1, source_target_pairs={{0,8},{8,0},{16,24},{24,16},{32,40},{40,32},{48,56},{56,48},{64,72... | collective-permute-start | bytes 393224 | tf_op jit(solution)/shard_map/ppermute | solution.py:367
  27.1 19.6 %collective-permute-start.35 = (bf16[1,2,256,128]{3,2,1,0:T(8,128)(2,1)S(1)}, bf16[1,2,256,128]{3,2,1,0:T(8,128)(2,1)S(1)}, u32[]{:S(2)}, u32[]{:S(2)}) collective-permute-start(bf16[1,2,256,128]{3,2,1,0:T(8,128)(2,1)S(1)} %select_bitcast_fusion.refs_0_), channel_id=1, source_target_pairs={{0,112},{8,120},{16,0},{24,8},{32,16},{40,24},{48,32},{56,40},{64,... | collective-permute-start | bytes 393224 | tf_op jit(solution)/shard_map/ppermute | solution.py:365
  36.2 10.5 %collective-permute-start.36 = (bf16[1,2,256,128]{3,2,1,0:T(8,128)(2,1)S(1)}, bf16[1,2,256,128]{3,2,1,0:T(8,128)(2,1)S(1)}, u32[]{:S(2)}, u32[]{:S(2)}) collective-permute-start(bf16[1,2,256,128]{3,2,1,0:T(8,128)(2,1)S(1)} %select_bitcast_fusion.refs_0_), channel_id=1, source_target_pairs={{0,16},{8,24},{16,32},{24,40},{32,48},{40,56},{48,64},{56,72},{64,... | collective-permute-start | bytes 393224 | tf_op jit(solution)/shard_map/ppermute | solution.py:366
  36.2 15.2 %collective-permute-start.37 = (bf16[1,2,256,128]{3,2,1,0:T(8,128)(2,1)S(1)}, bf16[1,2,256,128]{3,2,1,0:T(8,128)(2,1)S(1)}, u32[]{:S(2)}, u32[]{:S(2)}) collective-permute-start(bf16[1,2,256,128]{3,2,1,0:T(8,128)(2,1)S(1)} %select_bitcast_fusion.refs_0_), channel_id=1, source_target_pairs={{0,64},{8,72},{16,80},{24,88},{32,96},{40,104},{48,112},{56,120},{... | collective-permute-start | bytes 393224 | tf_op jit(solution)/shard_map/ppermute | solution.py:364
  51.5 5.7 %collective-permute-start.41 = (bf16[3,2,256,128]{3,2,1,0:T(8,128)(2,1)S(1)}, bf16[3,2,256,128]{3,2,1,0:T(8,128)(2,1)S(1)}, u32[]{:S(2)}, u32[]{:S(2)}) collective-permute-start(bf16[3,2,256,128]{3,2,1,0:T(8,128)(2,1)S(1)} %pad_maximum_fusion.1), channel_id=1, source_target_pairs={{0,8},{8,0},{16,24},{24,16},{32,40},{40,32},{48,56},{56,48},{64,72... | collective-permute-start | bytes 1179656 | tf_op jit(solution)/shard_map/ppermute | solution.py:373
  52.6 7.9 %collective-permute-start.39 = (bf16[2,2,256,128]{3,2,1,0:T(8,128)(2,1)S(1)}, bf16[2,2,256,128]{3,2,1,0:T(8,128)(2,1)S(1)}, u32[]{:S(2)}, u32[]{:S(2)}) collective-permute-start(bf16[2,2,256,128]{3,2,1,0:T(8,128)(2,1)S(1)} %get-tuple-element.246), channel_id=1, source_target_pairs={{0,112},{8,120},{16,0},{24,8},{32,16},{40,24},{48,32},{56,40},{64,... | collective-permute-start | bytes 786440 | tf_op jit(solution)/shard_map/ppermute | solution.py:371
  52.7 9.3 %collective-permute-start.40 = (bf16[2,2,256,128]{3,2,1,0:T(8,128)(2,1)S(1)}, bf16[2,2,256,128]{3,2,1,0:T(8,128)(2,1)S(1)}, u32[]{:S(2)}, u32[]{:S(2)}) collective-permute-start(bf16[2,2,256,128]{3,2,1,0:T(8,128)(2,1)S(1)} %get-tuple-element.245), channel_id=1, source_target_pairs={{0,16},{8,24},{16,32},{24,40},{32,48},{40,56},{48,64},{56,72},{64,... | collective-permute-start | bytes 786440 | tf_op jit(solution)/shard_map/ppermute | solution.py:372
  62.0 4.7 %collective-permute-start.42 = (bf16[4,2,256,128]{3,2,1,0:T(8,128)(2,1)S(1)}, bf16[4,2,256,128]{3,2,1,0:T(8,128)(2,1)S(1)}, u32[]{:S(2)}, u32[]{:S(2)}) collective-permute-start(bf16[4,2,256,128]{3,2,1,0:T(8,128)(2,1)S(1)} %pad_maximum_fusion), channel_id=1, source_target_pairs={{0,8},{8,0},{16,24},{24,16},{32,40},{40,32},{48,56},{56,48},{64,72... | collective-permute-start | bytes 1572872 | tf_op jit(solution)/shard_map/ppermute | solution.py:378
  73.3 9.1 %collective-permute-start.43 = (bf16[2,32,2048]{2,1,0:T(8,128)(2,1)S(1)}, bf16[2,32,2048]{2,1,0:T(8,128)(2,1)S(1)}, u32[]{:S(2)}, u32[]{:S(2)}) collective-permute-start(bf16[2,32,2048]{2,1,0:T(8,128)(2,1)S(1)} %get-tuple-element.235), channel_id=1, source_target_pairs={{0,1},{1,2},{2,3},{3,0},{4,5},{5,6},{6,7},{7,4},{8,9},{9,10},{10,1... | collective-permute-start | bytes 786440 | tf_op jit(solution)/shard_map/ppermute | solution.py:305
  74.6 7.9 %collective-permute-start.44 = (bf16[2,32,2048]{2,1,0:T(8,128)(2,1)S(1)}, bf16[2,32,2048]{2,1,0:T(8,128)(2,1)S(1)}, u32[]{:S(2)}, u32[]{:S(2)}) collective-permute-start(bf16[2,32,2048]{2,1,0:T(8,128)(2,1)S(1)} %get-tuple-element.236), channel_id=1, source_target_pairs={{0,3},{1,0},{2,1},{3,2},{4,7},{5,4},{6,5},{7,6},{8,11},{9,8},{10,9... | collective-permute-start | bytes 786440 | tf_op jit(solution)/shard_map/ppermute | solution.py:306
  76.0 13.0 %collective-permute-start.45 = (bf16[2,32,2048]{2,1,0:T(8,128)(2,1)S(1)}, bf16[2,32,2048]{2,1,0:T(8,128)(2,1)S(1)}, u32[]{:S(2)}, u32[]{:S(2)}) collective-permute-start(bf16[2,32,2048]{2,1,0:T(8,128)(2,1)S(1)} %get-tuple-element.237), channel_id=1, source_target_pairs={{0,2},{1,3},{2,0},{3,1},{4,6},{5,7},{6,4},{7,5},{8,10},{9,11},{10,... | collective-permute-start | bytes 786440 | tf_op jit(solution)/shard_map/ppermute | solution.py:304
  77.6 13.0 %collective-permute-start.47 = (bf16[4,32,2048]{2,1,0:T(8,128)(2,1)S(1)}, bf16[4,32,2048]{2,1,0:T(8,128)(2,1)S(1)}, u32[]{:S(2)}, u32[]{:S(2)}) collective-permute-start(bf16[4,32,2048]{2,1,0:T(8,128)(2,1)S(1)} %get-tuple-element.239), channel_id=1, source_target_pairs={{0,4},{1,5},{2,6},{3,7},{4,0},{5,1},{6,2},{7,3},{8,12},{9,13},{10,... | collective-permute-start | bytes 1572872 | tf_op jit(solution)/shard_map/ppermute | solution.py:302
  89.2 4.3 %collective-permute-start.46 = (bf16[32,2048]{1,0:T(8,128)(2,1)S(1)}, bf16[32,2048]{1,0:T(8,128)(2,1)S(1)}, u32[]{:S(2)}, u32[]{:S(2)}) collective-permute-start(bf16[32,2048]{1,0:T(8,128)(2,1)S(1)} %fusion.22), channel_id=1, source_target_pairs={{0,4},{1,5},{2,6},{3,7},{4,0},{5,1},{6,2},{7,3},{8,12},{9,13},{10,... | collective-permute-start | bytes 393224 | tf_op jit(solution)/shard_map/ppermute | solution.py:313
  90.7 5.1 %collective-permute-start.48 = (bf16[32,2048]{1,0:T(8,128)(2,1)S(1)}, bf16[32,2048]{1,0:T(8,128)(2,1)S(1)}, u32[]{:S(2)}, u32[]{:S(2)}) collective-permute-start(bf16[32,2048]{1,0:T(8,128)(2,1)S(1)} %get-tuple-element.242), channel_id=1, source_target_pairs={{0,1},{1,2},{2,3},{3,0},{4,5},{5,6},{6,7},{7,4},{8,9},{9,10},{10,1... | collective-permute-start | bytes 393224 | tf_op jit(solution)/shard_map/ppermute | solution.py:309
  91.4 5.8 %collective-permute-start.49 = (bf16[32,2048]{1,0:T(8,128)(2,1)S(1)}, bf16[32,2048]{1,0:T(8,128)(2,1)S(1)}, u32[]{:S(2)}, u32[]{:S(2)}) collective-permute-start(bf16[32,2048]{1,0:T(8,128)(2,1)S(1)} %get-tuple-element.244), channel_id=1, source_target_pairs={{0,3},{1,0},{2,1},{3,2},{4,7},{5,4},{6,5},{7,6},{8,11},{9,8},{10,9... | collective-permute-start | bytes 393224 | tf_op jit(solution)/shard_map/ppermute | solution.py:310
  93.5 5.6 %collective-permute-start.50 = (bf16[32,2048]{1,0:T(8,128)(2,1)S(1)}, bf16[32,2048]{1,0:T(8,128)(2,1)S(1)}, u32[]{:S(2)}, u32[]{:S(2)}) collective-permute-start(bf16[32,2048]{1,0:T(8,128)(2,1)S(1)} %get-tuple-element.243), channel_id=1, source_target_pairs={{0,2},{1,3},{2,0},{3,1},{4,6},{5,7},{6,4},{7,5},{8,10},{9,11},{10,... | collective-permute-start | bytes 393224 | tf_op jit(solution)/shard_map/ppermute | solution.py:311
  (6 other events, 139.0 us)
